TPU v7x, 32 devices: a whole 2x2x4 slice. The times are simulated.
32 devices in a mesh: data: 2 (over x), pp: 4 (over z), ep: 4 (over y, core).
Axes of the slice: x: 2, y: 2, z: 4, core: 2. Of those that a mesh axis runs over, the one named last changes fastest.
Arguments:
- expert_out: bfloat16 [4, 4, 512, 32, 2048], P('pp', 'data', 'ep'), parts along dimension 1
- expert_ids: int32 [4, 4, 4, 256, 10], P('pp', 'data', 'ep'), parts along dimension 1
- slot_ids: int32 [4, 4, 4, 256, 10], P('pp', 'data', 'ep'), parts along dimension 1
- gate_weights: float32 [4, 4, 4, 256, 10], P('pp', 'data', 'ep'), parts along dimension 1
- residual: bfloat16 [4, 4, 4, 256, 2048], P('pp', 'data', 'ep'), parts along dimension 1
- norm_moe: float32 [4, 2048], P('pp')
- w_gate: bfloat16 [4, 2048, 512], P('pp')
- w_up: bfloat16 [4, 2048, 512], P('pp')
- w_down: bfloat16 [4, 512, 2048], P('pp')
- norm_attn: float32 [4, 2048], P('pp')
- w_query: bfloat16 [4, 2048, 16, 256], P('pp')
- w_key: bfloat16 [4, 2048, 16, 256], P('pp')
- w_value: bfloat16 [4, 2048, 16, 256], P('pp')
- w_out: bfloat16 [4, 16, 256, 2048], P('pp')
Outputs:
- output: bfloat16 [4, 4, 4, 256, 2048], P('pp', 'data', 'ep'), parts along dimension 1
There are 2 independent parts. A program takes and returns all parts, laid end to end along the dimension named above; an argument that names none is the same for every part.
All inputs are finite; a program needn't handle non-finite values.
Results may differ from a plain program's by a relative error of at most 0.0163687.
Values are sent between devices in bfloat16 or wider.
A program may use at most 1 GiB of HBM per device.

v0:
```python
import math
import jax
import jax.numpy as jnp
from jax import lax
from jax.sharding import PartitionSpec as P

EPSILON = 1e-6


def rms_norm(tensor, gain):
    values = tensor.astype(jnp.float32)
    inv_rms = lax.rsqrt(jnp.mean(values * values, axis=-1, keepdims=True) + EPSILON)
    return values * inv_rms * gain


def shared_expert(residual, norm_moe, w_gate, w_up, w_down):
    normed = rms_norm(residual, norm_moe).astype(jnp.bfloat16)
    gate_act = jnp.einsum("bld,df->blf", normed, w_gate, preferred_element_type=jnp.float32)
    up_act = jnp.einsum("bld,df->blf", normed, w_up, preferred_element_type=jnp.float32)
    hidden = (jax.nn.silu(gate_act) * up_act).astype(jnp.bfloat16)
    return jnp.einsum("blf,fd->bld", hidden, w_down, preferred_element_type=jnp.float32).astype(jnp.bfloat16)


def gather_combine(row_table, row_ids, kept_mask, gate_weights):
    picked = jnp.take(row_table, row_ids, axis=0, mode="clip")
    weights = jnp.where(kept_mask, gate_weights, 0.0)
    return jnp.sum(picked.astype(jnp.float32) * weights[..., None], axis=-2)


def attention_block(combined, norm_attn, w_query, w_key, w_value, w_out):
    seq_len = combined.shape[1]
    score_scale = 1.0 / math.sqrt(w_query.shape[2])
    normed = rms_norm(combined, norm_attn).astype(jnp.bfloat16)
    queries = jnp.einsum("bld,dhe->blhe", normed, w_query, preferred_element_type=jnp.float32).astype(jnp.bfloat16)
    key_heads = jnp.einsum("bld,dhe->blhe", normed, w_key, preferred_element_type=jnp.float32).astype(jnp.bfloat16)
    value_heads = jnp.einsum("bld,dhe->blhe", normed, w_value, preferred_element_type=jnp.float32).astype(jnp.bfloat16)
    scores = jnp.einsum("bqhe,bkhe->bhqk", queries, key_heads, preferred_element_type=jnp.float32) * score_scale
    causal = jnp.arange(seq_len)[:, None] >= jnp.arange(seq_len)[None, :]
    scores = jnp.where(causal, scores, -1e30)
    attn_probs = jnp.exp(scores - jnp.max(scores, axis=-1, keepdims=True))
    prob_sum = jnp.sum(attn_probs, axis=-1, keepdims=True)
    attn_mixed = jnp.einsum("bhqk,bkhe->bhqe", attn_probs.astype(jnp.bfloat16), value_heads, preferred_element_type=jnp.float32) / prob_sum
    attn_proj = jnp.einsum("cirf,ife->cre", attn_mixed.astype(jnp.bfloat16), w_out, preferred_element_type=jnp.float32).astype(jnp.bfloat16)
    return (combined.astype(jnp.float32) + attn_proj.astype(jnp.float32)).astype(jnp.bfloat16)


def solution(mesh):
    stages = mesh.shape["pp"]
    ep_size = mesh.shape["ep"]
    shift_pairs = [(source, (source + 1) % stages) for source in range(stages)]
    tok_spec = P("pp", "data", "ep", None, None)
    vec_spec = P("pp", None)
    mat_spec = P("pp", None, None)
    head_spec = P("pp", None, None, None)

    def device_step(expert_out, expert_ids, slot_ids, gate_weights, residual, norm_moe, w_gate, w_up, w_down, norm_attn, w_query, w_key, w_value, w_out):
        micro_count = expert_out.shape[1]
        local_experts, slots_total, model_dim = expert_out.shape[2:]
        cap_slots = slots_total // ep_size
        first_slot = lax.axis_index("ep") * cap_slots
        results = []
        for micro_idx in range(micro_count):
            local_out = expert_out[0, micro_idx].reshape(local_experts, ep_size, cap_slots, model_dim)
            received = lax.all_to_all(local_out, "ep", 1, 0, tiled=True)
            row_table = received.reshape(local_experts * ep_size * cap_slots, model_dim)
            slot_here = slot_ids[0, micro_idx]
            kept_mask = slot_here >= 0
            row_ids = expert_ids[0, micro_idx] * cap_slots + jnp.where(kept_mask, slot_here - first_slot, 0)
            routed = gather_combine(row_table, row_ids, kept_mask, gate_weights[0, micro_idx])
            resid_here = residual[0, micro_idx]
            shared = shared_expert(resid_here, norm_moe[0], w_gate[0], w_up[0], w_down[0])
            combined = (resid_here.astype(jnp.float32) + shared.astype(jnp.float32) + routed).astype(jnp.bfloat16)
            incoming = lax.ppermute(combined, "pp", shift_pairs)
            results.append(attention_block(incoming, norm_attn[0], w_query[0], w_key[0], w_value[0], w_out[0]))
        return jnp.stack(results)[None]

    in_specs = (tok_spec,) * 5 + (vec_spec, mat_spec, mat_spec, mat_spec, vec_spec, head_spec, head_spec, head_spec, head_spec)
    return jax.shard_map(device_step, mesh=mesh, in_specs=in_specs, out_specs=tok_spec, check_vma=False)
```

profile of v0, /device:TPU:0, one launch (start us, length us, event | category | flops | bytes accessed | tf_op | source)
XLA Modules:
  0.0 611.0 jit_solution(15185338698014391929)
XLA Ops:
  0.0 18.5 %slice_bitcast_fusion.1 = (bf16[128,4,8,2048]{3,2,1,0:T(8,128)(2,1)}, bf16[128,4,8,2048]{3,2,1,0:T(8,128)(2,1)S(1)}) fusion(bf16[1,2,128,32,2048]{4,3,2,1,0:T(8,128)(2,1)} %param.14), kind=kLoop, calls=%fused_computation.9 | loop fusion | bytes 67108864 | tf_op jit(solution)/shard_map/reshape;squeeze | solution.py:63
  18.5 6.9 %copy.23 = bf16[128,4,8,2048]{3,2,0,1:T(8,128)(2,1)} copy(bf16[128,4,8,2048]{3,2,1,0:T(8,128)(2,1)S(1)} %get-tuple-element.10) | data formatting | bytes 33554432 | tf_op jit(solution)/shard_map/reshape;squeeze | solution.py:63
  25.5 7.0 %all-to-all-start.1 = ((bf16[128,4,8,2048]{3,2,0,1:T(8,128)(2,1)}), bf16[128,4,8,2048]{3,2,0,1:T(8,128)(2,1)}, u32[]{:S(2)}, u32[]{:S(2)}) async-start(bf16[128,4,8,2048]{3,2,0,1:T(8,128)(2,1)} %copy.23), calls=%async_computation.1 | async-start | bytes 33554432 | tf_op jit(solution)/shard_map/all_to_all | solution.py:64
  32.4 14.1 %copy.20 = bf16[128,4,8,2048]{3,2,0,1:T(8,128)(2,1)} copy(bf16[128,4,8,2048]{3,2,1,0:T(8,128)(2,1)} %get-tuple-element.9) | data formatting | bytes 33554432 | tf_op jit(solution)/shard_map/reshape;squeeze | solution.py:63
  46.5 169.4 %all-to-all-done.1 = bf16[128,4,8,2048]{3,2,0,1:T(8,128)(2,1)} async-done(((bf16[128,4,8,2048]{3,2,0,1:T(8,128)(2,1)}), bf16[128,4,8,2048]{3,2,0,1:T(8,128)(2,1)}, u32[]{:S(2)}, u32[]{:S(2)}) %all-to-all-start.1) | async-done | bytes 16777248 | tf_op jit(solution)/shard_map/all_to_all | solution.py:64
  215.9 7.1 %all-to-all-start = ((bf16[128,4,8,2048]{3,2,0,1:T(8,128)(2,1)}), bf16[128,4,8,2048]{3,2,0,1:T(8,128)(2,1)}, u32[]{:S(2)}, u32[]{:S(2)}) async-start(bf16[128,4,8,2048]{3,2,0,1:T(8,128)(2,1)} %copy.20), calls=%async_computation | async-start | bytes 33554432 | tf_op jit(solution)/shard_map/all_to_all | solution.py:64
  223.0 0.0 copy-start.11
  223.0 0.1 copy.34
  223.2 0.1 copy.21
  223.3 0.1 reshape.530
  223.5 0.1 copy.35
  223.6 0.1 copy.24
  223.7 0.1 reshape.538
  223.8 0.0 copy-start.3
  223.9 0.6 iota_compare_fusion
  224.5 2.0 fusion.78
  226.6 0.0 copy-start.10
  226.6 2.5 fusion.94
  229.1 1.6 fusion.96
  230.7 28.1 %gather_fusion.1 = bf16[2560,2048]{1,0:T(8,128)(2,1)} fusion(bf16[4096,2048]{1,0:T(8,128)(2,1)} %bitcast.27, s32[3072]{0:T(1024)S(1)} %pad_clamp_fusion), kind=kCustom, calls=%fused_computation.1 | custom fusion | bytes 20981760 | tf_op jit(solution)/shard_map/jit(_take)/gather | solution.py:25
  258.8 19.4 %reshape.545 = f32[1,256,10,2048]{3,2,1,0:T(8,128)} reshape(bf16[2560,2048]{1,0:T(8,128)(2,1)} %gather_fusion.1) | data formatting | bytes 31457280 | tf_op jit(solution)/shard_map/convert_element_type | solution.py:27
  278.2 15.5 %multiply_reduce_fusion = f32[256,2048]{1,0:T(8,128)} fusion(f32[1,256,10,2048]{3,2,1,0:T(8,128)} %reshape.545, f32[256,10]{1,0:T(8,128)S(1)} %bitcast.186), kind=kLoop, calls=%fused_computation.2 | loop fusion | flops 9961472 | bytes 23078912 | tf_op jit(solution)/shard_map/reduce_sum | solution.py:27
  293.7 5.2 fusion.70
  298.9 2.8 collective-permute-start.1
  301.7 104.0 %all-to-all-done = bf16[128,4,8,2048]{3,2,0,1:T(8,128)(2,1)} async-done(((bf16[128,4,8,2048]{3,2,0,1:T(8,128)(2,1)}), bf16[128,4,8,2048]{3,2,0,1:T(8,128)(2,1)}, u32[]{:S(2)}, u32[]{:S(2)}) %all-to-all-start) | async-done | bytes 16777248 | tf_op jit(solution)/shard_map/all_to_all | solution.py:64
  405.7 28.1 %gather_fusion = bf16[2560,2048]{1,0:T(8,128)(2,1)} fusion(bf16[4096,2048]{1,0:T(8,128)(2,1)} %bitcast.9, s32[3072]{0:T(1024)S(1)} %pad_clamp_fusion.1), kind=kCustom, calls=%fused_computation | custom fusion | bytes 20981760 | tf_op jit(solution)/shard_map/jit(_take)/gather | solution.py:25
  433.8 19.4 %reshape.544 = f32[1,256,10,2048]{3,2,1,0:T(8,128)} reshape(bf16[2560,2048]{1,0:T(8,128)(2,1)} %gather_fusion) | data formatting | bytes 31457280 | tf_op jit(solution)/shard_map/convert_element_type | solution.py:27
  453.2 15.5 %multiply_reduce_fusion.1 = f32[256,2048]{1,0:T(8,128)} fusion(f32[1,256,10,2048]{3,2,1,0:T(8,128)} %reshape.544, f32[256,10]{1,0:T(8,128)S(1)} %bitcast.185), kind=kLoop, calls=%fused_computation.3 | loop fusion | flops 9961472 | bytes 23078912 | tf_op jit(solution)/shard_map/reduce_sum | solution.py:27
  468.7 5.4 fusion.71
  474.1 2.5 collective-permute-start
  476.6 0.3 fusion.75
  476.9 11.3 %fusion.4 = bf16[256,16,256]{2,0,1:T(8,128)(2,1)S(1)} fusion(bf16[2048,16,256]{2,1,0:T(8,128)(2,1)} %bitcast.187, bf16[1,256,2048]{2,1,0:T(8,128)(2,1)S(1)} %collective-permute-done.1, f32[256]{0:T(256)S(1)} %add_rsqrt_fusion, f32[2048]{0:T(1024)S(1)} %bitcast.197), kind=kOutput, calls=%fused_computation.10 | convolution fusion | flops 4297064448 | bytes 19932160 | tf_op jit(solution)/shard_map/bld,dhe->blhe/dot_general | solution.py:36
  488.2 2.5 copy.62
  490.8 11.3 %collective-permute-done = bf16[1,256,2048]{2,1,0:T(8,128)(2,1)S(1)} collective-permute-done((bf16[1,256,2048]{2,1,0:T(8,128)(2,1)}, bf16[1,256,2048]{2,1,0:T(8,128)(2,1)S(1)}, u32[]{:S(2)}, u32[]{:S(2)}) %collective-permute-start) | collective-permute-done | bytes 1048608 | tf_op jit(solution)/shard_map/ppermute | solution.py:73
  502.1 0.3 fusion.72
  502.4 11.6 %fusion.6 = bf16[256,16,256]{2,0,1:T(8,128)(2,1)S(1)} fusion(bf16[2048,16,256]{2,1,0:T(8,128)(2,1)} %bitcast.188, bf16[1,256,2048]{2,1,0:T(8,128)(2,1)S(1)} %collective-permute-done, f32[2048]{0:T(1024)S(1)} %bitcast.198, f32[256]{0:T(256)S(1)} %add_rsqrt_fusion.2), kind=kOutput, calls=%fused_computation.12 | convolution fusion | flops 4297064448 | bytes 19932160 | tf_op jit(solution)/shard_map/bld,dhe->blhe/dot_general | solution.py:36
  514.0 2.6 copy.63
  516.6 12.7 %fusion.14 = bf16[256,16,256]{2,0,1:T(8,128)(2,1)} fusion(bf16[2048,16,256]{2,1,0:T(8,128)(2,1)} %bitcast.189, bf16[1,256,2048]{2,1,0:T(8,128)(2,1)S(1)} %collective-permute-done, f32[2048]{0:T(1024)S(1)} %bitcast.199, f32[256]{0:T(256)S(1)} %add_rsqrt_fusion.2), kind=kOutput, calls=%fused_computation.20 | convolution fusion | flops 4297064448 | bytes 19932160 | tf_op jit(solution)/shard_map/bld,dhe->blhe/dot_general | solution.py:34
  529.3 15.5 %fusion.16 = (f32[16,256]{1,0:T(8,128)S(1)}, f32[16,256,256]{1,2,0:T(8,128)}) fusion(pred[256,256]{0,1:T(8,128)(4,1)S(1)} %copy-done.4, bf16[256,16,256]{2,0,1:T(8,128)(2,1)} %fusion.14, bf16[2048,16,256]{2,1,0:T(8,128)(2,1)} %bitcast.191, bf16[1,256,2048]{2,1,0:T(8,128)(2,1)} %copy-done.5, f32[2048]{0:T(1024)S(1)} %bitcast.200, f32[256]{0:T(256)S(1)} %add_rsqrt_fusion.2), kind=kOutput, calls=%fused_computation.30 | convolution fusion | flops 4838125568 | bytes 24208384 | tf_op jit(solution)/shard_map/bqhe,bkhe->bhqk/dot_general | solution.py:37
  544.8 6.8 %fusion.86 = f32[16,256,256]{2,1,0:T(8,128)} fusion(f32[16,256,256]{1,2,0:T(8,128)} %get-tuple-element.16, bf16[256,16,256]{2,1,0:T(8,128)(2,1)} %copy.63, f32[16,256]{1,0:T(8,128)S(1)} %get-tuple-element.15, pred[256,256]{0,1:T(8,128)(4,1)S(1)} %copy-done.4), kind=kOutput, calls=%fused_computation.85 | convolution fusion | flops 541065216 | bytes 10567680 | tf_op jit(solution)/shard_map/bhqk,bkhe->bhqe/dot_general | solution.py:42
  551.5 12.7 %fusion.12 = bf16[256,16,256]{2,0,1:T(8,128)(2,1)} fusion(bf16[2048,16,256]{2,1,0:T(8,128)(2,1)} %bitcast.190, bf16[1,256,2048]{2,1,0:T(8,128)(2,1)S(1)} %collective-permute-done.1, f32[256]{0:T(256)S(1)} %add_rsqrt_fusion, f32[2048]{0:T(1024)S(1)} %bitcast.201), kind=kOutput, calls=%fused_computation.18 | convolution fusion | flops 4297064448 | bytes 19932160 | tf_op jit(solution)/shard_map/bld,dhe->blhe/dot_general | solution.py:34
  564.2 16.9 %fusion.18 = (f32[16,256]{1,0:T(8,128)S(1)}, f32[16,256]{1,0:T(8,128)S(1)}, f32[16,256,256]{1,2,0:T(8,128)}) fusion(f32[16,256,256]{1,2,0:T(8,128)} %get-tuple-element.16, f32[16,256]{1,0:T(8,128)S(1)} %get-tuple-element.15, pred[256,256]{0,1:T(8,128)(4,1)S(1)} %copy-done.4, bf16[256,16,256]{2,0,1:T(8,128)(2,1)} %fusion.12, ...), kind=kOutput, calls=%fused_computation.32 | convolution fusion | flops 4842315776 | bytes 28435456 | tf_op jit(solution)/shard_map/bqhe,bkhe->bhqk/dot_general | solution.py:37
  581.1 3.2 fusion.20
  584.3 0.2 copy-done.1
  584.6 3.9 fusion.84
  588.5 10.4 %fusion.53 = bf16[1,1,256,2048]{3,2,1,0:T(8,128)(2,1)S(1)} fusion(bf16[1,16,256,2048]{3,2,1,0:T(8,128)(2,1)} %param.27, bf16[1,256,2048]{2,1,0:T(8,128)(2,1)S(1)} %copy-done.6, f32[16,256,256]{2,1,0:T(8,128)S(1)} %copy-done.2, f32[16,256]{1,0:T(8,128)S(1)} %get-tuple-element.7), kind=kOutput, calls=%fused_computation.65 | convolution fusion | flops 4299685888 | bytes 23085056 | tf_op jit(solution)/shard_map/cirf,ife->cre/dot_general | solution.py:43
  598.9 10.4 %fusion.67 = bf16[1,1,256,2048]{3,2,1,0:T(8,128)(2,1)S(1)} fusion(bf16[1,16,256,2048]{3,2,1,0:T(8,128)(2,1)} %param.27, bf16[1,256,2048]{2,1,0:T(8,128)(2,1)S(1)} %collective-permute-done.1, f32[16,256,256]{2,1,0:T(8,128)S(1)} %fusion.84, f32[16,256]{1,0:T(8,128)S(1)} %fusion.20), kind=kOutput, calls=%fused_computation.69 | convolution fusion | flops 4299685888 | bytes 23085056 | tf_op jit(solution)/shard_map/cirf,ife->cre/dot_general | solution.py:43
  609.3 1.5 maximum_bitcast_fusion
  (31 shorter events, 0.2 us)
Async XLA Ops:
  0.0 293.7 %copy-start = (bf16[1,512,2048]{2,1,0:T(8,128)(2,1)S(1)}, bf16[1,512,2048]{2,1,0:T(8,128)(2,1)}, u32[]{:S(2)}) copy-start(bf16[1,512,2048]{2,1,0:T(8,128)(2,1)} %param.22) | copy-start | bytes 6291460
  25.5 190.4 %all-to-all-start.1 = ((bf16[128,4,8,2048]{3,2,0,1:T(8,128)(2,1)}), bf16[128,4,8,2048]{3,2,0,1:T(8,128)(2,1)}, u32[]{:S(2)}, u32[]{:S(2)}) async-start(bf16[128,4,8,2048]{3,2,0,1:T(8,128)(2,1)} %copy.23), calls=%async_computation.1 | async-start | bytes 33554432 | tf_op jit(solution)/shard_map/all_to_all | solution.py:64
  46.5 176.5 %copy-start.7 = (s32[1,2,1,256,10]{3,2,4,1,0:T(1,128)S(1)}, s32[1,2,1,256,10]{3,2,4,1,0:T(1,128)}, u32[]{:S(2)}) copy-start(s32[1,2,1,256,10]{3,2,4,1,0:T(1,128)} %param.16) | copy-start | bytes 61444
  46.5 176.5 %copy-start.9 = (f32[1,2,1,256,10]{3,2,4,1,0:T(1,128)S(1)}, f32[1,2,1,256,10]{3,2,4,1,0:T(1,128)}, u32[]{:S(2)}) copy-start(f32[1,2,1,256,10]{3,2,4,1,0:T(1,128)} %param.17) | copy-start | bytes 61444
  46.5 176.6 %copy-start.8 = (s32[1,2,1,256,10]{3,2,4,1,0:T(1,128)S(1)}, s32[1,2,1,256,10]{3,2,4,1,0:T(1,128)}, u32[]{:S(2)}) copy-start(s32[1,2,1,256,10]{3,2,4,1,0:T(1,128)} %param.15) | copy-start | bytes 61444
  215.9 189.8 %all-to-all-start = ((bf16[128,4,8,2048]{3,2,0,1:T(8,128)(2,1)}), bf16[128,4,8,2048]{3,2,0,1:T(8,128)(2,1)}, u32[]{:S(2)}, u32[]{:S(2)}) async-start(bf16[128,4,8,2048]{3,2,0,1:T(8,128)(2,1)} %copy.20), calls=%async_computation | async-start | bytes 33554432 | tf_op jit(solution)/shard_map/all_to_all | solution.py:64
  223.0 3.6 copy-start.11
  223.8 2.7 copy-start.3
  226.6 2.5 copy-start.10
  298.9 177.7 %collective-permute-start.1 = (bf16[1,256,2048]{2,1,0:T(8,128)(2,1)}, bf16[1,256,2048]{2,1,0:T(8,128)(2,1)S(1)}, u32[]{:S(2)}, u32[]{:S(2)}) collective-permute-start(bf16[1,256,2048]{2,1,0:T(8,128)(2,1)} %fusion.70), channel_id=1, source_target_pairs={{0,4},{4,8},{8,12},{12,0},{1,5},{5,9},{9,13},{13,1},{2,6},{6,10},{... | collective-permute-start | bytes 3145736 | tf_op jit(solution)/shard_map/ppermute | solution.py:73
  468.7 8.2 %copy-start.12 = (f32[1,2048]{1,0:T(1,128)S(1)}, f32[1,2048]{1,0:T(1,128)}, u32[]{:S(2)}) copy-start(f32[1,2048]{1,0:T(1,128)} %param.23) | copy-start | bytes 24580
  474.1 27.9 %collective-permute-start = (bf16[1,256,2048]{2,1,0:T(8,128)(2,1)}, bf16[1,256,2048]{2,1,0:T(8,128)(2,1)S(1)}, u32[]{:S(2)}, u32[]{:S(2)}) collective-permute-start(bf16[1,256,2048]{2,1,0:T(8,128)(2,1)} %fusion.71), channel_id=1, source_target_pairs={{0,4},{4,8},{8,12},{12,0},{1,5},{5,9},{9,13},{13,1},{2,6},{6,10},{... | collective-permute-start | bytes 3145736 | tf_op jit(solution)/shard_map/ppermute | solution.py:73
  502.1 14.5 %copy-start.5 = (bf16[1,256,2048]{2,1,0:T(8,128)(2,1)}, bf16[1,256,2048]{2,1,0:T(8,128)(2,1)S(1)}, u32[]{:S(2)}) copy-start(bf16[1,256,2048]{2,1,0:T(8,128)(2,1)S(1)} %collective-permute-done) | copy-start | bytes 3145732
  516.6 12.7 %copy-start.4 = (pred[256,256]{0,1:T(8,128)(4,1)S(1)}, pred[256,256]{0,1:T(8,128)(4,1)}, u32[]{:S(2)}) copy-start(pred[256,256]{0,1:T(8,128)(4,1)} %iota_compare_fusion) | copy-start | bytes 196612
  581.1 3.4 copy-start.1
  584.6 3.9 copy-start.2
  584.6 3.9 copy-start.6
where the time goes:
time: 620 us; the launch traced here: 611 us
  waiting for transfers between devices  285 us (46%)
  local copies, waits for them, and re-layouts  141 us (23%)
  matrix products  127 us (20%)
  other arithmetic  39 us (6%)
  starting transfers between devices  19.3 us (3%)
    all_to_all x2, waiting for transfers between devices, device_step(): received = lax.all_to_all(local_out, 'ep', 1, 0, tiled=True)  273 us
    gather x2, local copies, waits for them, and re-layouts, gather_combine(): picked = jnp.take(row_table, row_ids, axis=0, mode='clip')  56.2 us
    another operation x3, local copies, waits for them, and re-layouts, device_step(): expert_out[0, micro_idx]  39.5 us
    convert_element_type x2, local copies, waits for them, and re-layouts, gather_combine(): return jnp.sum(picked.astype(jnp.float32) * weights[..., None], axis=-2)  38.9 us
    dot_general x2, matrix products, attention_block(): jnp.einsum('bqhe,bkhe->bhqk', queries, key_heads, preferred_element_type=...  32.4 us
    reduce_sum x2, other arithmetic, gather_combine(): return jnp.sum(picked.astype(jnp.float32) * weights[..., None], axis=-2)  31 us
    dot_general x2, matrix products, attention_block(): jnp.einsum('bld,dhe->blhe', normed, w_query, preferred_element_type=jnp.f...  25.4 us
    dot_general x2, matrix products, attention_block(): jnp.einsum('bld,dhe->blhe', normed, w_value, preferred_element_type=jnp.f...  22.9 us
  transfers between devices with their start and end apart: 4, of which 3 were waited for; matrix products, arithmetic and copies ran while one was open for 28% of the time, Pallas kernels for 0%

commit v1 on v0

v1 whole, which is shorter than its diff:
```python
import functools

import jax
import jax.numpy as jnp
from jax import lax
from jax.experimental import pallas as pl
from jax.experimental.pallas import tpu as pltpu
from jax.sharding import PartitionSpec as P

EPSILON = 1e-6
MESH = pl.DeviceIdType.MESH
F32, BF16 = jnp.float32, jnp.bfloat16
BF16_MAX = 3.3895313892515355e38
META_ROWS = 32
GATE_ROW = 16


def boundary_kernel(dims, meta, rows_hbm, resid_hbm, norm_moe, norm_attn, wg_hbm, wu_hbm, wd_hbm, wq_hbm, wk_hbm, wv_hbm, wo_hbm,
                    out_hbm, wrel_hbm,
                    meta_all, meta_cols, send_part, recv_part, mine, y_recv, recv_own, acc, y_send, y_in, resid,
                    meta_ss, meta_rs, part_ss, part_rs, own_ss, own_rs, y_ss, y_rs, z_ss, z_rs, row_sem, misc_sem, w_sem, o_sem, rl_in, rl_out):
    micro, seq, model, heads, head_dim, local_experts, cap, top_k, ff, stages = dims
    local_cols = local_experts * cap
    half = seq // 2
    piece = 32
    pieces = seq // piece
    per_half = half // piece

    me = lax.axis_index("ep")
    stage = lax.axis_index("pp")
    chip, core = me // 2, me % 2
    partner = chip * 2 + (1 - core)
    across = (1 - chip) * 2 + core
    diag = (1 - chip) * 2 + (1 - core)
    nxt, prv = (stage + 1) % stages, (stage + stages - 1) % stages

    barrier = pltpu.get_barrier_semaphore()
    for peer in (partner, across, diag):
        pl.semaphore_signal(barrier, inc=1, device_id={"ep": peer}, device_id_type=MESH)
    for peer in (nxt, prv):
        pl.semaphore_signal(barrier, inc=1, device_id={"pp": peer}, device_id_type=MESH)
    pl.semaphore_wait(barrier, 5)

    def meta_copy(rel, peer):
        return pltpu.make_async_remote_copy(src_ref=meta, dst_ref=meta_all.at[rel - 1], send_sem=meta_ss.at[rel - 1], recv_sem=meta_rs.at[rel - 1], device_id={"ep": peer}, device_id_type=MESH)

    def part_copy(m, c):
        sl = pl.ds(pl.multiple_of(c * half, half), half)
        return pltpu.make_async_remote_copy(src_ref=send_part.at[m, sl], dst_ref=recv_part.at[m, sl], send_sem=part_ss.at[m, c], recv_sem=part_rs.at[m, c], device_id={"ep": partner}, device_id_type=MESH)

    def own_copy(m, c):
        sl = pl.ds(pl.multiple_of(c * half, half), half)
        return pltpu.make_async_remote_copy(src_ref=send_part.at[m, sl], dst_ref=recv_own.at[m, sl], send_sem=own_ss.at[m, c], recv_sem=own_rs.at[m, c], device_id={"ep": partner}, device_id_type=MESH)

    def y_copy(m, k):
        sl = pl.ds(pl.multiple_of(k * piece, piece), piece)
        return pltpu.make_async_remote_copy(src_ref=mine.at[m, sl], dst_ref=y_recv.at[m, sl], send_sem=y_ss.at[m, k], recv_sem=y_rs.at[m, k], device_id={"ep": across}, device_id_type=MESH)

    def z_copy(m, k):
        sl = pl.ds(pl.multiple_of(k * piece, piece), piece)
        return pltpu.make_async_remote_copy(src_ref=y_send.at[m, sl], dst_ref=y_in.at[m, sl], send_sem=z_ss.at[m, k], recv_sem=z_rs.at[m, k], device_id={"pp": nxt}, device_id_type=MESH)

    for rel, peer in ((2, across), (3, diag), (1, partner)):
        meta_copy(rel, peer).start()

    def phase_one(rbuf, wbuf, wg, wu, wd, xs, hid):
        def rows_copy(p, ab):
            m = p % 2
            far = 1 - p // 2
            owner_a = far * diag + (1 - far) * partner
            owner_b = far * across + (1 - far) * me
            owner = owner_a if ab == 0 else owner_b
            src = rows_hbm.at[m, :, pl.ds(pl.multiple_of(owner * cap, cap), cap), :]
            return pltpu.make_async_copy(src, rbuf.at[p % 2, ab], row_sem.at[p % 2, ab])

        rows_copy(0, 0).start()
        rows_copy(0, 1).start()
        res_cp = pltpu.make_async_copy(resid_hbm, resid, misc_sem.at[0])
        wg_cp = pltpu.make_async_copy(wg_hbm, wg, misc_sem.at[1])
        wu_cp = pltpu.make_async_copy(wu_hbm, wu, misc_sem.at[2])
        wd_cp = pltpu.make_async_copy(wd_hbm, wd, misc_sem.at[3])
        for cp in (res_cp, wg_cp, wu_cp, wd_cp):
            cp.start()

        for m in range(micro):
            meta_cols[0, m] = meta[m].T
        for rel, peer in ((2, across), (3, diag), (1, partner)):
            meta_copy(rel, peer).wait()
            for m in range(micro):
                meta_cols[rel, m] = meta_all[rel - 1, m].T

        base = (local_cols * me).astype(F32)
        lane = lax.broadcasted_iota(jnp.int32, (half, 256), 1).astype(F32) + base

        def partial_sum(p, c, ab, dst):
            m = p % 2
            far = 1 - p // 2
            rel = (1 + 2 * far) if ab == 0 else 2 * far
            tok = pl.ds(pl.multiple_of(c * half, half), half)
            table = meta_cols[rel, m, tok, :]

            def build(kb, carry):
                col_id = lane + (kb * 256).astype(F32)
                w = jnp.zeros((half, 256), F32)
                for j in range(top_k):
                    w = jnp.where(table[:, j:j + 1] == col_id, table[:, GATE_ROW + j:GATE_ROW + j + 1], w)
                hi = jnp.minimum(w, BF16_MAX).astype(BF16)
                rest = w - hi.astype(F32)
                mid = rest.astype(BF16)
                low = (rest - mid.astype(F32)).astype(BF16)
                kk = pl.ds(pl.multiple_of(kb * 256, 256), 256)
                wbuf[ab, 0:half, kk] = hi
                wbuf[ab, half:2 * half, kk] = mid
                wbuf[ab, 2 * half:3 * half, kk] = low
                return carry

            lax.fori_loop(0, local_cols // 256, build, 0)

            def mul(n, carry):
                nn = pl.ds(pl.multiple_of(n * 512, 512), 512)
                rr = rbuf[p % 2, ab, :, :, nn].reshape(local_cols, 512)
                d = jnp.dot(wbuf[ab], rr, preferred_element_type=F32)
                dst[m, tok, nn] = d[0:half] + d[half:2 * half] + d[2 * half:3 * half]
                return carry

            lax.fori_loop(0, model // 512, mul, 0)

        def pair_step(q, carry):
            p, c = q // 2, q % 2
            m = p % 2

            @pl.when(c == 0)
            def _():
                rows_copy(p, 0).wait()
                rows_copy(p, 1).wait()

                @pl.when(p < 3)
                def _():
                    rows_copy(p + 1, 0).start()
                    rows_copy(p + 1, 1).start()

            @pl.when(p >= 2)
            def _():
                part_copy(m, c).wait_send()

            partial_sum(p, c, 0, send_part)

            @pl.when(p < 2)
            def _():
                part_copy(m, c).start()

            @pl.when(p >= 2)
            def _():
                own_copy(m, c).start()

            @pl.when(p < 2)
            def _():
                partial_sum(p, c, 1, mine)
                part_copy(m, c).wait_recv()

                def add(k, carry):
                    sl = pl.ds(pl.multiple_of(k * piece, piece), piece)
                    mine[m, sl] = mine[m, sl] + recv_part[m, sl]
                    y_copy(m, k).start()
                    return carry

                lax.fori_loop(c * per_half, (c + 1) * per_half, add, 0)

            @pl.when(p >= 2)
            def _():
                partial_sum(p, c, 1, acc)
            return carry

        lax.fori_loop(0, 8, pair_step, 0)

        for cp in (res_cp, wg_cp, wu_cp, wd_cp):
            cp.wait()

        def shared(m, carry):
            def norm(k, carry):
                sl = pl.ds(pl.multiple_of(k * piece, piece), piece)
                v = resid[m, sl].astype(F32)
                inv = lax.rsqrt(jnp.mean(v * v, axis=-1, keepdims=True) + EPSILON)
                xs[sl] = (v * inv * norm_moe[...]).astype(BF16)
                return carry

            lax.fori_loop(0, pieces, norm, 0)

            def up(n, carry):
                nn = pl.ds(pl.multiple_of(n * 256, 256), 256)
                g = jnp.dot(xs[...], wg[:, nn], preferred_element_type=F32)
                u = jnp.dot(xs[...], wu[:, nn], preferred_element_type=F32)
                hid[:, nn] = (g * (1.0 / (1.0 + jnp.exp(-g))) * u).astype(BF16)
                return carry

            lax.fori_loop(0, ff // 256, up, 0)
            for c in range(2):
                own_copy(m, c).wait()

            def down(n, carry):
                nn = pl.ds(pl.multiple_of(n * 256, 256), 256)
                s = jnp.dot(hid[...], wd[:, nn], preferred_element_type=F32).astype(BF16)
                acc[m, :, nn] = (resid[m, :, nn].astype(F32) + s.astype(F32)) + (acc[m, :, nn] + recv_own[m, :, nn])
                return carry

            lax.fori_loop(0, model // 256, down, 0)
            return carry

        lax.fori_loop(0, micro, shared, 0)

    pl.run_scoped(
        phase_one,
        pltpu.VMEM((2, 2, local_experts, cap, model), BF16),
        pltpu.VMEM((2, 3 * half, local_cols), BF16),
        pltpu.VMEM((model, ff), BF16),
        pltpu.VMEM((model, ff), BF16),
        pltpu.VMEM((ff, model), BF16),
        pltpu.VMEM((seq, model), BF16),
        pltpu.VMEM((seq, ff), BF16),
    )

    def finish(m, lo, hi):
        def body(k, carry):
            sl = pl.ds(pl.multiple_of(k * piece, piece), piece)
            y_copy(m, k).wait()
            y_send[m, sl] = (acc[m, sl] + y_recv[m, sl]).astype(BF16)
            z_copy(m, k).start()
            return carry

        lax.fori_loop(lo, hi, body, 0)

    def phase_two(rin, rout, wbuf, obuf, wob, xbuf, mixed):
        d_blk = 64
        sub = 256 // heads
        blocks = model // d_blk
        row = lax.broadcasted_iota(jnp.int32, (256, 256), 0)
        col = lax.broadcasted_iota(jnp.int32, (256, 256), 1)
        pick = jnp.where(col == (row % sub) * heads + row // sub, 1.0, 0.0).astype(BF16)

        def relayout(mat, src_hbm):
            def in_copy(b):
                return pltpu.make_async_copy(src_hbm.at[pl.ds(pl.multiple_of(b * d_blk, d_blk), d_blk)], rin.at[b % 2], rl_in.at[b % 2])

            def out_copy(b):
                return pltpu.make_async_copy(rout.at[b % 2], wrel_hbm.at[mat, :, pl.ds(pl.multiple_of(b * d_blk, d_blk), d_blk), :], rl_out.at[b % 2])

            in_copy(0).start()

            def body(b, carry):
                in_copy(b).wait()

                @pl.when(b + 1 < blocks)
                def _():
                    in_copy(b + 1).start()

                @pl.when(b >= 2)
                def _():
                    out_copy(b - 2).wait()
                for i in range(d_blk // sub):
                    tile = rin[b % 2, i * sub:(i + 1) * sub].reshape(sub * heads, head_dim)
                    moved = jnp.dot(pick, tile, preferred_element_type=F32).astype(BF16)
                    rout[b % 2, :, i * sub:(i + 1) * sub, :] = moved.reshape(heads, sub, head_dim)
                out_copy(b).start()
                return carry

            lax.fori_loop(0, blocks, body, 0)
            out_copy(blocks - 2).wait()
            out_copy(blocks - 1).wait()

        finish(0, 0, 4)
        relayout(0, wq_hbm)
        finish(0, 4, 6)
        relayout(1, wk_hbm)
        finish(0, 6, 8)
        relayout(2, wv_hbm)

        def w_copy(h, mat):
            return pltpu.make_async_copy(wrel_hbm.at[mat, h], wbuf.at[h % 2, mat], w_sem.at[h % 2, mat])

        n_out = model // 512

        def o_copy(n):
            return pltpu.make_async_copy(wo_hbm.at[:, pl.ds(pl.multiple_of(n * 512, 512), 512)], wob.at[n % 2], o_sem.at[n % 2])

        for mat in range(3):
            w_copy(0, mat).start()
        o_copy(0).start()

        qi = lax.broadcasted_iota(jnp.int32, (seq, seq), 0)
        ki = lax.broadcasted_iota(jnp.int32, (seq, seq), 1)
        causal = qi >= ki
        scale = 1.0 / (head_dim ** 0.5)

        def attention(m):
            last = m == micro - 1

            def norm(k, carry):
                sl = pl.ds(pl.multiple_of(k * piece, piece), piece)
                z_copy(m, k).wait()
                v = y_in[m, sl].astype(F32)
                inv = lax.rsqrt(jnp.mean(v * v, axis=-1, keepdims=True) + EPSILON)
                xbuf[sl] = (v * inv * norm_attn[...]).astype(BF16)
                return carry

            lax.fori_loop(0, pieces, norm, 0)

            def head(h, carry):
                slot = h % 2
                for mat in range(3):
                    w_copy(h, mat).wait()

                def prefetch():
                    for mat in range(3):
                        w_copy((h + 1) % heads, mat).start()

                if last:
                    pl.when(h + 1 < heads)(prefetch)
                else:
                    prefetch()
                x = xbuf[...]
                q = jnp.dot(x, wbuf[slot, 0], preferred_element_type=F32).astype(BF16)
                k = jnp.dot(x, wbuf[slot, 1], preferred_element_type=F32).astype(BF16)
                v = jnp.dot(x, wbuf[slot, 2], preferred_element_type=F32).astype(BF16)
                s = lax.dot_general(q, k, (((1,), (1,)), ((), ())), preferred_element_type=F32) * scale
                s = jnp.where(causal, s, -1e30)
                e = jnp.exp(s - jnp.max(s, axis=-1, keepdims=True))
                total = jnp.sum(e, axis=-1, keepdims=True)
                o = jnp.dot(e.astype(BF16), v, preferred_element_type=F32) / total
                mixed[:, pl.ds(pl.multiple_of(h * head_dim, head_dim), head_dim)] = o.astype(BF16)
                if not last:
                    @pl.when((h % 4 == 0) & (h > 0))
                    def _():
                        finish(1, h // 4 + 1, h // 4 + 2)
                return carry

            lax.fori_loop(0, heads, head, 0)

            def proj(n, carry):
                nn = pl.ds(pl.multiple_of(n * 512, 512), 512)
                o_copy(n).wait()
                if last:
                    pl.when(n + 1 < n_out)(lambda: o_copy(n + 1).start())
                else:
                    o_copy((n + 1) % n_out).start()
                pr = jnp.dot(mixed[...], wob[n % 2], preferred_element_type=F32).astype(BF16)
                obuf[m, :, nn] = (y_in[m, :, nn].astype(F32) + pr.astype(F32)).astype(BF16)
                return carry

            lax.fori_loop(0, n_out, proj, 0)
            pltpu.make_async_copy(obuf.at[m], out_hbm.at[m], misc_sem.at[4 + m]).start()

        finish(1, 0, 2)
        attention(0)
        finish(1, 5, 8)
        attention(1)
        for m in range(micro):
            pltpu.make_async_copy(obuf.at[m], out_hbm.at[m], misc_sem.at[4 + m]).wait()

    pl.run_scoped(
        phase_two,
        pltpu.VMEM((2, 64, heads, head_dim), BF16),
        pltpu.VMEM((2, heads, 64, head_dim), BF16),
        pltpu.VMEM((2, 3, model, head_dim), BF16),
        pltpu.VMEM((micro, seq, model), BF16),
        pltpu.VMEM((2, heads * head_dim, 512), BF16),
        pltpu.VMEM((seq, model), BF16),
        pltpu.VMEM((seq, heads * head_dim), BF16),
    )


def solution(mesh):
    stages = mesh.shape["pp"]
    ep_size = mesh.shape["ep"]
    tok_spec = P("pp", "data", "ep", None, None)
    vec_spec = P("pp", None)
    mat_spec = P("pp", None, None)
    head_spec = P("pp", None, None, None)

    def device_step(expert_out, expert_ids, slot_ids, gate_weights, residual, norm_moe, w_gate, w_up, w_down, norm_attn, w_query, w_key, w_value, w_out):
        micro = expert_out.shape[1]
        local_experts, slots_total, model = expert_out.shape[2:]
        cap = slots_total // ep_size
        seq, top_k = expert_ids.shape[3:]
        heads, head_dim = w_query.shape[2:]
        ff = w_gate.shape[2]
        ids = jnp.swapaxes(expert_ids[0, :, 0], 1, 2)
        slots = jnp.swapaxes(slot_ids[0, :, 0], 1, 2)
        gates = jnp.swapaxes(gate_weights[0, :, 0], 1, 2)
        kept = slots >= 0
        cols = jnp.where(kept, ids * cap + (slots - lax.axis_index("ep") * cap), -1).astype(F32)
        gates = jnp.where(kept, gates, 0.0)
        gap = ((0, 0), (0, GATE_ROW - top_k), (0, 0))
        meta = jnp.concatenate([jnp.pad(cols, gap), jnp.pad(gates, gap)], axis=1)

        dims = (micro, seq, model, heads, head_dim, local_experts, cap, top_k, ff, stages)
        hbm = pl.BlockSpec(memory_space=pl.ANY)
        vmem = pl.BlockSpec(memory_space=pltpu.VMEM)
        dma = pltpu.SemaphoreType.DMA
        pieces = seq // 32
        out, _ = pl.pallas_call(
            functools.partial(boundary_kernel, dims),
            out_shape=(jax.ShapeDtypeStruct((micro, seq, model), BF16), jax.ShapeDtypeStruct((3, heads, model, head_dim), BF16)),
            in_specs=[vmem, hbm, hbm, vmem, vmem] + [hbm] * 7,
            out_specs=(hbm, hbm),
            scratch_shapes=[
                pltpu.VMEM((3, micro, META_ROWS, seq), F32),
                pltpu.VMEM((4, micro, seq, META_ROWS), F32),
                pltpu.VMEM((micro, seq, model), F32),
                pltpu.VMEM((micro, seq, model), F32),
                pltpu.VMEM((micro, seq, model), F32),
                pltpu.VMEM((micro, seq, model), F32),
                pltpu.VMEM((micro, seq, model), F32),
                pltpu.VMEM((micro, seq, model), F32),
                pltpu.VMEM((micro, seq, model), BF16),
                pltpu.VMEM((micro, seq, model), BF16),
                pltpu.VMEM((micro, seq, model), BF16),
                dma((3,)), dma((3,)),
                dma((micro, 2)), dma((micro, 2)),
                dma((micro, 2)), dma((micro, 2)),
                dma((micro, pieces)), dma((micro, pieces)),
                dma((micro, pieces)), dma((micro, pieces)),
                dma((2, 2)), dma((6,)), dma((2, 3)), dma((2,)), dma((2,)), dma((2,)),
            ],
            compiler_params=pltpu.CompilerParams(collective_id=0, has_side_effects=True, vmem_limit_bytes=67043328),
        )(
            meta,
            expert_out[0],
            residual[0, :, 0],
            norm_moe, norm_attn,
            w_gate[0], w_up[0], w_down[0],
            w_query[0], w_key[0], w_value[0],
            w_out[0].reshape(heads * head_dim, model),
        )
        return out[None, :, None]

    in_specs = (tok_spec,) * 5 + (vec_spec, mat_spec, mat_spec, mat_spec, vec_spec, head_spec, head_spec, head_spec, head_spec)
    return jax.shard_map(device_step, mesh=mesh, in_specs=in_specs, out_specs=tok_spec, check_vma=False)
```

time: 620 us -> 290 us (0.47)
  waiting for transfers between devices: 285 us -> 0 us
  Pallas kernels: 0 us -> 280 us
  local copies, waits for them, and re-layouts: 141 us -> 3.16 us
  matrix products: 127 us -> 0 us
  other arithmetic: 39 us -> 2.15 us
  starting transfers between devices: 19.3 us -> 0 us
    pallas_call x0 -> x1, Pallas kernels: none -> 280 us  [device_step(): pl.pallas_call(functools.partial(boundary_kernel, dims), out_shape=(jax.S...]
    all_to_all x2 -> x0, waiting for transfers between devices: 273 us -> none  [device_step(): received = lax.all_to_all(local_out, 'ep', 1, 0, tiled=True)]
    dot_general x14 -> x0, matrix products: 127 us -> none  [the longest x2 32.4 us: attention_block(): jnp.einsum('bqhe,bkhe->bhqk', queries, key_heads, preferred_element_type=...]
    gather x2 -> x0, local copies, waits for them, and re-layouts: 56.2 us -> none  [gather_combine(): picked = jnp.take(row_table, row_ids, axis=0, mode='clip')]
    another operation x3 -> x0, local copies, waits for them, and re-layouts: 39.5 us -> none  [device_step(): expert_out[0, micro_idx]]
    convert_element_type x2 -> x0, local copies, waits for them, and re-layouts: 38.9 us -> none  [gather_combine(): return jnp.sum(picked.astype(jnp.float32) * weights[..., None], axis=-2)]
    reduce_sum x6 -> x0, other arithmetic: 36.8 us -> none  [the longest x2 31 us: gather_combine(): return jnp.sum(picked.astype(jnp.float32) * weights[..., None], axis=-2)]
    all_to_all x2 -> x0, starting transfers between devices: 14 us -> none  [device_step(): received = lax.all_to_all(local_out, 'ep', 1, 0, tiled=True)]
  transfers between devices with their start and end apart: 4 -> 0, of which waited for: 3 -> 0; matrix products, arithmetic and copies ran while one was open for 28% -> 0% of each run, Pallas kernels for 0% -> 0%
where the time goes in v1:
time: 290 us; the launch traced here: 285 us
  Pallas kernels  280 us (97%)
  local copies, waits for them, and re-layouts  3.16 us (1%)
    pallas_call x1, Pallas kernels, device_step(): pl.pallas_call(functools.partial(boundary_kernel, dims), out_shape=(jax.S...  280 us

profile of v1, /device:TPU:0, one launch (start us, length us, event | category | flops | bytes accessed | tf_op | source)
XLA Modules:
  0.0 285.0 jit_solution(4829786088050743894)
XLA Ops:
  0.0 0.8 fusion.3
  0.8 0.8 fusion.4
  1.5 0.6 select_maximum_fusion.meta
  2.2 279.7 %shard_map.136 = (bf16[2,256,2048]{2,1,0:T(8,128)(2,1)}, bf16[3,16,2048,256]{3,2,1,0:T(8,128)(2,1)}) custom-call(f32[2,32,256]{2,1,0:T(8,128)} %select_maximum_fusion.meta, bf16[2,128,32,2048]{3,2,1,0:T(8,128)(2,1)} %bitcast.20, bf16[2,256,2048]{2,1,0:T(8,128)(2,1)} %bitcast.25, f32[1,2048]{1,0:T(1,128)} %norm_moe.1, f32[1,2048]{1,0:T(1,128)} %norm_attn.1, ...), custom_call_target="tpu_custom_call" | custom-call | tf_op jit(solution)/shard_map/pallas_call | solution.py:400
  281.8 3.2 %copy.41 = bf16[1,2,1,256,2048]{4,3,2,1,0:T(8,128)(2,1)} copy(bf16[1,2,1,256,2048]{4,3,2,1,0:T(8,128)(2,1)} %bitcast.29) | data formatting | bytes 4194304

commit v2 on v1

--- a/solution.py
+++ b/solution.py
@@ -11,13 +11,15 @@
 MESH = pl.DeviceIdType.MESH
 F32, BF16 = jnp.float32, jnp.bfloat16
 BF16_MAX = 3.3895313892515355e38
-META_ROWS = 32
+META_ROWS = 48
 GATE_ROW = 16
+SLOT_ROW = 32
+RIN, ROUT, WSLOTS, OSLOTS, OCOLS = 6, 3, 4, 4, 256
 
 
 def boundary_kernel(dims, meta, rows_hbm, resid_hbm, norm_moe, norm_attn, wg_hbm, wu_hbm, wd_hbm, wq_hbm, wk_hbm, wv_hbm, wo_hbm,
                     out_hbm, wrel_hbm,
-                    meta_all, meta_cols, send_part, recv_part, mine, y_recv, recv_own, acc, y_send, y_in, resid,
+                    meta_all, meta_cols, send_part, recv_part, mine, y_recv, recv_own, acc, y_send, y_in,
                     meta_ss, meta_rs, part_ss, part_rs, own_ss, own_rs, y_ss, y_rs, z_ss, z_rs, row_sem, misc_sem, w_sem, o_sem, rl_in, rl_out):
     micro, seq, model, heads, head_dim, local_experts, cap, top_k, ff, stages = dims
     local_cols = local_experts * cap
@@ -63,7 +65,7 @@
     for rel, peer in ((2, across), (3, diag), (1, partner)):
         meta_copy(rel, peer).start()
 
-    def phase_one(rbuf, wbuf, wg, wu, wd, xs, hid):
+    def phase_one(rbuf, wbuf, wg, wu, wd, xs, hid, resid, spread):
         def rows_copy(p, ab):
             m = p % 2
             far = 1 - p // 2
@@ -89,8 +91,12 @@
             for m in range(micro):
                 meta_cols[rel, m] = meta_all[rel - 1, m].T
 
-        base = (local_cols * me).astype(F32)
-        lane = lax.broadcasted_iota(jnp.int32, (half, 256), 1).astype(F32) + base
+        lane = (lax.broadcasted_iota(jnp.int32, (half, local_experts), 1) + local_experts * me).astype(F32)
+        lane_slot = (lax.broadcasted_iota(jnp.int32, (half, 256), 1) % cap).astype(F32)
+        from_row = lax.broadcasted_iota(jnp.int32, (local_experts, 256), 0)
+        to_col = lax.broadcasted_iota(jnp.int32, (local_experts, 256), 1) // cap
+        for kb in range(local_cols // 256):
+            spread[kb] = jnp.where(from_row == to_col + kb * (256 // cap), 1.0, 0.0).astype(BF16)
 
         def partial_sum(p, c, ab, dst):
             m = p % 2
@@ -99,22 +105,23 @@
             tok = pl.ds(pl.multiple_of(c * half, half), half)
             table = meta_cols[rel, m, tok, :]
 
-            def build(kb, carry):
-                col_id = lane + (kb * 256).astype(F32)
-                w = jnp.zeros((half, 256), F32)
-                for j in range(top_k):
-                    w = jnp.where(table[:, j:j + 1] == col_id, table[:, GATE_ROW + j:GATE_ROW + j + 1], w)
-                hi = jnp.minimum(w, BF16_MAX).astype(BF16)
-                rest = w - hi.astype(F32)
-                mid = rest.astype(BF16)
-                low = (rest - mid.astype(F32)).astype(BF16)
-                kk = pl.ds(pl.multiple_of(kb * 256, 256), 256)
-                wbuf[ab, 0:half, kk] = hi
-                wbuf[ab, half:2 * half, kk] = mid
-                wbuf[ab, 2 * half:3 * half, kk] = low
-                return carry
-
-            lax.fori_loop(0, local_cols // 256, build, 0)
+            gate = jnp.zeros((half, local_experts), F32)
+            slot = jnp.zeros((half, local_experts), F32)
+            for j in range(top_k):
+                hit = table[:, j:j + 1] == lane
+                gate = jnp.where(hit, table[:, GATE_ROW + j:GATE_ROW + j + 1], gate)
+                slot = jnp.where(hit, table[:, SLOT_ROW + j:SLOT_ROW + j + 1], slot)
+            hi = jnp.minimum(gate, BF16_MAX).astype(BF16)
+            rest = gate - hi.astype(F32)
+            mid = rest.astype(BF16)
+            low = (rest - mid.astype(F32)).astype(BF16)
+            packed = jnp.concatenate([slot.astype(BF16), hi, mid, low], axis=0)
+            for kb in range(local_cols // 256):
+                wide = jnp.dot(packed, spread[kb], preferred_element_type=F32)
+                keep = wide[0:half] == lane_slot
+                for part in range(3):
+                    term = jnp.where(keep, wide[(part + 1) * half:(part + 2) * half], 0.0)
+                    wbuf[ab, part * half:(part + 1) * half, kb * 256:(kb + 1) * 256] = term.astype(BF16)
 
             def mul(n, carry):
                 nn = pl.ds(pl.multiple_of(n * 512, 512), 512)
@@ -217,6 +224,8 @@
         pltpu.VMEM((ff, model), BF16),
         pltpu.VMEM((seq, model), BF16),
         pltpu.VMEM((seq, ff), BF16),
+        pltpu.VMEM((micro, seq, model), BF16),
+        pltpu.VMEM((local_cols // 256, local_experts, 256), BF16),
     )
 
     def finish(m, lo, hi):
@@ -239,33 +248,34 @@
 
         def relayout(mat, src_hbm):
             def in_copy(b):
-                return pltpu.make_async_copy(src_hbm.at[pl.ds(pl.multiple_of(b * d_blk, d_blk), d_blk)], rin.at[b % 2], rl_in.at[b % 2])
+                return pltpu.make_async_copy(src_hbm.at[pl.ds(pl.multiple_of(b * d_blk, d_blk), d_blk)], rin.at[b % RIN], rl_in.at[b % RIN])
 
             def out_copy(b):
-                return pltpu.make_async_copy(rout.at[b % 2], wrel_hbm.at[mat, :, pl.ds(pl.multiple_of(b * d_blk, d_blk), d_blk), :], rl_out.at[b % 2])
-
-            in_copy(0).start()
+                return pltpu.make_async_copy(rout.at[b % ROUT], wrel_hbm.at[mat, :, pl.ds(pl.multiple_of(b * d_blk, d_blk), d_blk), :], rl_out.at[b % ROUT])
+
+            for b in range(RIN - 1):
+                in_copy(b).start()
 
             def body(b, carry):
                 in_copy(b).wait()
 
-                @pl.when(b + 1 < blocks)
+                @pl.when(b + RIN - 1 < blocks)
                 def _():
-                    in_copy(b + 1).start()
-
-                @pl.when(b >= 2)
+                    in_copy(b + RIN - 1).start()
+
+                @pl.when(b >= ROUT)
                 def _():
-                    out_copy(b - 2).wait()
+                    out_copy(b - ROUT).wait()
                 for i in range(d_blk // sub):
-                    tile = rin[b % 2, i * sub:(i + 1) * sub].reshape(sub * heads, head_dim)
+                    tile = rin[b % RIN, i * sub:(i + 1) * sub].reshape(sub * heads, head_dim)
                     moved = jnp.dot(pick, tile, preferred_element_type=F32).astype(BF16)
-                    rout[b % 2, :, i * sub:(i + 1) * sub, :] = moved.reshape(heads, sub, head_dim)
+                    rout[b % ROUT, :, i * sub:(i + 1) * sub, :] = moved.reshape(heads, sub, head_dim)
                 out_copy(b).start()
                 return carry
 
             lax.fori_loop(0, blocks, body, 0)
-            out_copy(blocks - 2).wait()
-            out_copy(blocks - 1).wait()
+            for b in range(blocks - ROUT, blocks):
+                out_copy(b).wait()
 
         finish(0, 0, 4)
         relayout(0, wq_hbm)
@@ -275,16 +285,18 @@
         relayout(2, wv_hbm)
 
         def w_copy(h, mat):
-            return pltpu.make_async_copy(wrel_hbm.at[mat, h], wbuf.at[h % 2, mat], w_sem.at[h % 2, mat])
-
-        n_out = model // 512
+            return pltpu.make_async_copy(wrel_hbm.at[mat, h], wbuf.at[h % WSLOTS, mat], w_sem.at[h % WSLOTS, mat])
+
+        n_out = model // OCOLS
 
         def o_copy(n):
-            return pltpu.make_async_copy(wo_hbm.at[:, pl.ds(pl.multiple_of(n * 512, 512), 512)], wob.at[n % 2], o_sem.at[n % 2])
-
-        for mat in range(3):
-            w_copy(0, mat).start()
-        o_copy(0).start()
+            return pltpu.make_async_copy(wo_hbm.at[:, pl.ds(pl.multiple_of(n * OCOLS, OCOLS), OCOLS)], wob.at[n % OSLOTS], o_sem.at[n % OSLOTS])
+
+        for h in range(WSLOTS - 1):
+            for mat in range(3):
+                w_copy(h, mat).start()
+        for n in range(OSLOTS - 1):
+            o_copy(n).start()
 
         qi = lax.broadcasted_iota(jnp.int32, (seq, seq), 0)
         ki = lax.broadcasted_iota(jnp.int32, (seq, seq), 1)
@@ -305,16 +317,16 @@
             lax.fori_loop(0, pieces, norm, 0)
 
             def head(h, carry):
-                slot = h % 2
+                slot = h % WSLOTS
                 for mat in range(3):
                     w_copy(h, mat).wait()
 
                 def prefetch():
                     for mat in range(3):
-                        w_copy((h + 1) % heads, mat).start()
+                        w_copy((h + WSLOTS - 1) % heads, mat).start()
 
                 if last:
-                    pl.when(h + 1 < heads)(prefetch)
+                    pl.when(h + WSLOTS - 1 < heads)(prefetch)
                 else:
                     prefetch()
                 x = xbuf[...]
@@ -336,33 +348,33 @@
             lax.fori_loop(0, heads, head, 0)
 
             def proj(n, carry):
-                nn = pl.ds(pl.multiple_of(n * 512, 512), 512)
+                nn = pl.ds(pl.multiple_of(n * OCOLS, OCOLS), OCOLS)
                 o_copy(n).wait()
                 if last:
-                    pl.when(n + 1 < n_out)(lambda: o_copy(n + 1).start())
+                    pl.when(n + OSLOTS - 1 < n_out)(lambda: o_copy(n + OSLOTS - 1).start())
                 else:
-                    o_copy((n + 1) % n_out).start()
-                pr = jnp.dot(mixed[...], wob[n % 2], preferred_element_type=F32).astype(BF16)
-                obuf[m, :, nn] = (y_in[m, :, nn].astype(F32) + pr.astype(F32)).astype(BF16)
+                    o_copy((n + OSLOTS - 1) % n_out).start()
+                pr = jnp.dot(mixed[...], wob[n % OSLOTS], preferred_element_type=F32).astype(BF16)
+                obuf[:, nn] = (y_in[m, :, nn].astype(F32) + pr.astype(F32)).astype(BF16)
                 return carry
 
             lax.fori_loop(0, n_out, proj, 0)
-            pltpu.make_async_copy(obuf.at[m], out_hbm.at[m], misc_sem.at[4 + m]).start()
+            out_cp = pltpu.make_async_copy(obuf, out_hbm.at[m], misc_sem.at[4])
+            out_cp.start()
+            out_cp.wait()
 
         finish(1, 0, 2)
         attention(0)
         finish(1, 5, 8)
         attention(1)
-        for m in range(micro):
-            pltpu.make_async_copy(obuf.at[m], out_hbm.at[m], misc_sem.at[4 + m]).wait()
 
     pl.run_scoped(
         phase_two,
-        pltpu.VMEM((2, 64, heads, head_dim), BF16),
-        pltpu.VMEM((2, heads, 64, head_dim), BF16),
-        pltpu.VMEM((2, 3, model, head_dim), BF16),
-        pltpu.VMEM((micro, seq, model), BF16),
-        pltpu.VMEM((2, heads * head_dim, 512), BF16),
+        pltpu.VMEM((RIN, 64, heads, head_dim), BF16),
+        pltpu.VMEM((ROUT, heads, 64, head_dim), BF16),
+        pltpu.VMEM((WSLOTS, 3, model, head_dim), BF16),
+        pltpu.VMEM((seq, model), BF16),
+        pltpu.VMEM((OSLOTS, heads * head_dim, OCOLS), BF16),
         pltpu.VMEM((seq, model), BF16),
         pltpu.VMEM((seq, heads * head_dim), BF16),
     )
@@ -387,10 +399,10 @@
         slots = jnp.swapaxes(slot_ids[0, :, 0], 1, 2)
         gates = jnp.swapaxes(gate_weights[0, :, 0], 1, 2)
         kept = slots >= 0
-        cols = jnp.where(kept, ids * cap + (slots - lax.axis_index("ep") * cap), -1).astype(F32)
-        gates = jnp.where(kept, gates, 0.0)
+        experts = jnp.where(kept, ids, -1).astype(F32)
+        own_slots = (slots - lax.axis_index("ep") * cap).astype(F32)
         gap = ((0, 0), (0, GATE_ROW - top_k), (0, 0))
-        meta = jnp.concatenate([jnp.pad(cols, gap), jnp.pad(gates, gap)], axis=1)
+        meta = jnp.concatenate([jnp.pad(a, gap) for a in (experts, gates, own_slots)], axis=1)
 
         dims = (micro, seq, model, heads, head_dim, local_experts, cap, top_k, ff, stages)
         hbm = pl.BlockSpec(memory_space=pl.ANY)
@@ -413,13 +425,12 @@
                 pltpu.VMEM((micro, seq, model), F32),
                 pltpu.VMEM((micro, seq, model), BF16),
                 pltpu.VMEM((micro, seq, model), BF16),
-                pltpu.VMEM((micro, seq, model), BF16),
                 dma((3,)), dma((3,)),
                 dma((micro, 2)), dma((micro, 2)),
                 dma((micro, 2)), dma((micro, 2)),
                 dma((micro, pieces)), dma((micro, pieces)),
                 dma((micro, pieces)), dma((micro, pieces)),
-                dma((2, 2)), dma((6,)), dma((2, 3)), dma((2,)), dma((2,)), dma((2,)),
+                dma((2, 2)), dma((5,)), dma((WSLOTS, 3)), dma((OSLOTS,)), dma((RIN,)), dma((ROUT,)),
             ],
             compiler_params=pltpu.CompilerParams(collective_id=0, has_side_effects=True, vmem_limit_bytes=67043328),
         )(

time: 290 us -> 193 us (0.67); the launches traced: 285 us -> 193 us
  Pallas kernels: 280 us -> 187 us
    pallas_call x1, Pallas kernels: 280 us -> 187 us  [device_step(): pl.pallas_call(functools.partial(boundary_kernel, dims), out_shape=(jax.S...]
where the time goes in v2:
time: 193 us
  Pallas kernels  187 us (97%)
  local copies, waits for them, and re-layouts  3.9 us (2%)
    pallas_call x1, Pallas kernels, device_step(): pl.pallas_call(functools.partial(boundary_kernel, dims), out_shape=(jax.S...  187 us
    unnamed x2, local copies, waits for them, and re-layouts  3.9 us

profile of v2, /device:TPU:0, one launch (start us, length us, event | category | flops | bytes accessed | tf_op | source)
XLA Modules:
  0.0 192.7 jit_solution(2091746188678843679)
XLA Ops:
  0.0 0.7 copy.41
  0.8 0.8 fusion.4
  1.5 0.6 select_maximum_fusion.meta
  2.2 187.4 %shard_map.136 = (bf16[2,256,2048]{2,1,0:T(8,128)(2,1)}, bf16[3,16,2048,256]{3,2,1,0:T(8,128)(2,1)}) custom-call(f32[2,48,256]{2,1,0:T(8,128)} %select_maximum_fusion.meta, bf16[2,128,32,2048]{3,2,1,0:T(8,128)(2,1)} %bitcast.26, bf16[2,256,2048]{2,1,0:T(8,128)(2,1)} %bitcast.31, f32[1,2048]{1,0:T(1,128)} %norm_moe.1, f32[1,2048]{1,0:T(1,128)} %norm_attn.1, ...), custom_call_target="tpu_custom_call" | custom-call | tf_op jit(solution)/shard_map/pallas_call | solution.py:412
  189.5 3.2 %copy.43 = bf16[1,2,1,256,2048]{4,3,2,1,0:T(8,128)(2,1)} copy(bf16[1,2,1,256,2048]{4,3,2,1,0:T(8,128)(2,1)} %bitcast.35) | data formatting | bytes 4194304
  (1 shorter events, 0.0 us)

commit v3 on v2

--- a/solution.py
+++ b/solution.py
@@ -14,7 +14,7 @@
 META_ROWS = 48
 GATE_ROW = 16
 SLOT_ROW = 32
-RIN, ROUT, WSLOTS, OSLOTS, OCOLS = 6, 3, 4, 4, 256
+RIN, ROUT, D_BLK, WSLOTS, OROWS = 6, 4, 64, 4, 1024
 
 
 def boundary_kernel(dims, meta, rows_hbm, resid_hbm, norm_moe, norm_attn, wg_hbm, wu_hbm, wd_hbm, wq_hbm, wk_hbm, wv_hbm, wo_hbm,
@@ -65,7 +65,17 @@
     for rel, peer in ((2, across), (3, diag), (1, partner)):
         meta_copy(rel, peer).start()
 
-    def phase_one(rbuf, wbuf, wg, wu, wd, xs, hid, resid, spread):
+    def finish(m, lo, hi):
+        def body(k, carry):
+            sl = pl.ds(pl.multiple_of(k * piece, piece), piece)
+            y_copy(m, k).wait()
+            y_send[m, sl] = (acc[m, sl] + y_recv[m, sl]).astype(BF16)
+            z_copy(m, k).start()
+            return carry
+
+        lax.fori_loop(lo, hi, body, 0)
+
+    def phase_one(rbuf, wbuf, wg, wu, wd, xs, hid, resid, spread, pick, rin, rout):
         def rows_copy(p, ab):
             m = p % 2
             far = 1 - p // 2
@@ -73,7 +83,8 @@
             owner_b = far * across + (1 - far) * me
             owner = owner_a if ab == 0 else owner_b
             src = rows_hbm.at[m, :, pl.ds(pl.multiple_of(owner * cap, cap), cap), :]
-            return pltpu.make_async_copy(src, rbuf.at[p % 2, ab], row_sem.at[p % 2, ab])
+            at = (2 * p + ab) % 3
+            return pltpu.make_async_copy(src, rbuf.at[at], row_sem.at[at])
 
         rows_copy(0, 0).start()
         rows_copy(0, 1).start()
@@ -91,48 +102,88 @@
             for m in range(micro):
                 meta_cols[rel, m] = meta_all[rel - 1, m].T
 
-        lane = (lax.broadcasted_iota(jnp.int32, (half, local_experts), 1) + local_experts * me).astype(F32)
-        lane_slot = (lax.broadcasted_iota(jnp.int32, (half, 256), 1) % cap).astype(F32)
+        group = 32
+        lane = (lax.broadcasted_iota(jnp.int32, (group, local_experts), 1) + local_experts * me).astype(F32)
+        lane_slot = (lax.broadcasted_iota(jnp.int32, (group, 256), 1) % cap).astype(F32)
         from_row = lax.broadcasted_iota(jnp.int32, (local_experts, 256), 0)
         to_col = lax.broadcasted_iota(jnp.int32, (local_experts, 256), 1) // cap
         for kb in range(local_cols // 256):
             spread[kb] = jnp.where(from_row == to_col + kb * (256 // cap), 1.0, 0.0).astype(BF16)
 
-        def partial_sum(p, c, ab, dst):
+        sub = 256 // heads
+        mat_blocks = model // D_BLK
+        row = lax.broadcasted_iota(jnp.int32, (256, 256), 0)
+        col = lax.broadcasted_iota(jnp.int32, (256, 256), 1)
+        pick[...] = jnp.where(col == (row % sub) * heads + row // sub, 1.0, 0.0).astype(BF16)
+
+        def in_copy(src, b):
+            at = pl.ds(pl.multiple_of(b % mat_blocks * D_BLK, D_BLK), D_BLK)
+            return pltpu.make_async_copy(src.at[at], rin.at[b % RIN], rl_in.at[b % RIN])
+
+        def in_start(b):
+            for mat, src in enumerate((wq_hbm, wk_hbm, wv_hbm)):
+                pl.when(b // mat_blocks == mat)(lambda: in_copy(src, b).start())
+
+        def out_copy(b):
+            at = pl.ds(pl.multiple_of(b % mat_blocks * D_BLK, D_BLK), D_BLK)
+            return pltpu.make_async_copy(rout.at[b % ROUT], wrel_hbm.at[b // mat_blocks, :, at, :], rl_out.at[b % ROUT])
+
+        for b in range(RIN - 2):
+            in_copy(wq_hbm, b).start()
+
+        def partial_sum(p, c, ab, dst, ride=False):
             m = p % 2
             far = 1 - p // 2
             rel = (1 + 2 * far) if ab == 0 else 2 * far
             tok = pl.ds(pl.multiple_of(c * half, half), half)
             table = meta_cols[rel, m, tok, :]
 
-            gate = jnp.zeros((half, local_experts), F32)
-            slot = jnp.zeros((half, local_experts), F32)
-            for j in range(top_k):
-                hit = table[:, j:j + 1] == lane
-                gate = jnp.where(hit, table[:, GATE_ROW + j:GATE_ROW + j + 1], gate)
-                slot = jnp.where(hit, table[:, SLOT_ROW + j:SLOT_ROW + j + 1], slot)
-            hi = jnp.minimum(gate, BF16_MAX).astype(BF16)
-            rest = gate - hi.astype(F32)
-            mid = rest.astype(BF16)
-            low = (rest - mid.astype(F32)).astype(BF16)
-            packed = jnp.concatenate([slot.astype(BF16), hi, mid, low], axis=0)
-            for kb in range(local_cols // 256):
-                wide = jnp.dot(packed, spread[kb], preferred_element_type=F32)
-                keep = wide[0:half] == lane_slot
-                for part in range(3):
-                    term = jnp.where(keep, wide[(part + 1) * half:(part + 2) * half], 0.0)
-                    wbuf[ab, part * half:(part + 1) * half, kb * 256:(kb + 1) * 256] = term.astype(BF16)
+            for r in range(half // group):
+                rows = slice(r * group, (r + 1) * group)
+                gate = jnp.zeros((group, local_experts), F32)
+                slot = jnp.zeros((group, local_experts), F32)
+                for j in range(top_k):
+                    hit = table[rows, j:j + 1] == lane
+                    gate = jnp.where(hit, table[rows, GATE_ROW + j:GATE_ROW + j + 1], gate)
+                    slot = jnp.where(hit, table[rows, SLOT_ROW + j:SLOT_ROW + j + 1], slot)
+                hi = jnp.minimum(gate, BF16_MAX).astype(BF16)
+                rest = gate - hi.astype(F32)
+                mid = rest.astype(BF16)
+                low = (rest - mid.astype(F32)).astype(BF16)
+                packed = jnp.concatenate([slot.astype(BF16), hi, mid, low], axis=0)
+                for kb in range(local_cols // 256):
+                    wide = jnp.dot(packed, spread[kb], preferred_element_type=F32)
+                    keep = wide[0:group] == lane_slot
+                    for part in range(3):
+                        term = jnp.where(keep, wide[(part + 1) * group:(part + 2) * group], 0.0)
+                        wbuf[ab, part * half + r * group:part * half + (r + 1) * group, kb * 256:(kb + 1) * 256] = term.astype(BF16)
 
             def mul(n, carry):
                 nn = pl.ds(pl.multiple_of(n * 512, 512), 512)
-                rr = rbuf[p % 2, ab, :, :, nn].reshape(local_cols, 512)
+                b0 = 2 * (((2 * p + c - 2) * 2 + ab) * (model // 512) + n)
+                if ride:
+                    for b in (b0, b0 + 1):
+                        in_copy(wq_hbm, b).wait()
+                        in_start(b + RIN - 2)
+
+                        @pl.when(b >= ROUT)
+                        def _():
+                            out_copy(b - ROUT).wait()
+                rr = rbuf[(2 * p + ab) % 3, :, :, nn].reshape(local_cols, 512)
                 d = jnp.dot(wbuf[ab], rr, preferred_element_type=F32)
                 dst[m, tok, nn] = d[0:half] + d[half:2 * half] + d[2 * half:3 * half]
+                if ride:
+                    for b in (b0, b0 + 1):
+                        for i in range(D_BLK // sub):
+                            tile = rin[b % RIN, i * sub:(i + 1) * sub].reshape(sub * heads, head_dim)
+                            moved = jnp.dot(pick[...], tile, preferred_element_type=F32).astype(BF16)
+                            rout[b % ROUT, :, i * sub:(i + 1) * sub, :] = moved.reshape(heads, sub, head_dim)
+                        out_copy(b).start()
                 return carry
 
             lax.fori_loop(0, model // 512, mul, 0)
 
-        def pair_step(q, carry):
+        def pair_step(q, ride):
             p, c = q // 2, q % 2
             m = p % 2
 
@@ -140,29 +191,17 @@
             def _():
                 rows_copy(p, 0).wait()
                 rows_copy(p, 1).wait()
-
-                @pl.when(p < 3)
-                def _():
-                    rows_copy(p + 1, 0).start()
-                    rows_copy(p + 1, 1).start()
-
-            @pl.when(p >= 2)
-            def _():
-                part_copy(m, c).wait_send()
-
-            partial_sum(p, c, 0, send_part)
+                pl.when(p < 3)(lambda: rows_copy(p + 1, 0).start())
+
+            pl.when(p >= 2)(lambda: part_copy(m, c).wait_send())
+            partial_sum(p, c, 0, send_part, ride)
+            pl.when((p < 3) & (c == 1))(lambda: rows_copy(p + 1, 1).start())
+            pl.when(p < 2)(lambda: part_copy(m, c).start())
+            pl.when(p >= 2)(lambda: own_copy(m, c).start())
 
             @pl.when(p < 2)
             def _():
-                part_copy(m, c).start()
-
-            @pl.when(p >= 2)
-            def _():
-                own_copy(m, c).start()
-
-            @pl.when(p < 2)
-            def _():
-                partial_sum(p, c, 1, mine)
+                partial_sum(p, c, 1, mine, ride)
                 part_copy(m, c).wait_recv()
 
                 def add(k, carry):
@@ -173,17 +212,10 @@
 
                 lax.fori_loop(c * per_half, (c + 1) * per_half, add, 0)
 
-            @pl.when(p >= 2)
-            def _():
-                partial_sum(p, c, 1, acc)
-            return carry
-
-        lax.fori_loop(0, 8, pair_step, 0)
-
-        for cp in (res_cp, wg_cp, wu_cp, wd_cp):
-            cp.wait()
-
-        def shared(m, carry):
+            if ride:
+                pl.when(p >= 2)(lambda: partial_sum(p, c, 1, acc, ride))
+
+        def shared(m):
             def norm(k, carry):
                 sl = pl.ds(pl.multiple_of(k * piece, piece), piece)
                 v = resid[m, sl].astype(F32)
@@ -211,13 +243,39 @@
                 return carry
 
             lax.fori_loop(0, model // 256, down, 0)
+
+        def stage_step(t, carry):
+            def riding(c, inner):
+                pair_step(2 * t + c, True)
+                return inner
+
+            lax.fori_loop(0, 2, riding, 0)
+
+            @pl.when(t >= 2)
+            def _():
+                @pl.when(t == 2)
+                def _():
+                    for cp in (res_cp, wg_cp, wu_cp, wd_cp):
+                        cp.wait()
+                shared(t - 2)
+
+                @pl.when(t == 2)
+                def _():
+                    finish(0, 0, 6)
             return carry
 
-        lax.fori_loop(0, micro, shared, 0)
+        def first(q, carry):
+            pair_step(q, False)
+            return carry
+
+        lax.fori_loop(0, 2, first, 0)
+        lax.fori_loop(1, 4, stage_step, 0)
+        for b in range(3 * mat_blocks - ROUT, 3 * mat_blocks):
+            out_copy(b).wait()
 
     pl.run_scoped(
         phase_one,
-        pltpu.VMEM((2, 2, local_experts, cap, model), BF16),
+        pltpu.VMEM((3, local_experts, cap, model), BF16),
         pltpu.VMEM((2, 3 * half, local_cols), BF16),
         pltpu.VMEM((model, ff), BF16),
         pltpu.VMEM((model, ff), BF16),
@@ -226,77 +284,24 @@
         pltpu.VMEM((seq, ff), BF16),
         pltpu.VMEM((micro, seq, model), BF16),
         pltpu.VMEM((local_cols // 256, local_experts, 256), BF16),
+        pltpu.VMEM((256, 256), BF16),
+        pltpu.VMEM((RIN, D_BLK, heads, head_dim), BF16),
+        pltpu.VMEM((ROUT, heads, D_BLK, head_dim), BF16),
     )
 
-    def finish(m, lo, hi):
-        def body(k, carry):
-            sl = pl.ds(pl.multiple_of(k * piece, piece), piece)
-            y_copy(m, k).wait()
-            y_send[m, sl] = (acc[m, sl] + y_recv[m, sl]).astype(BF16)
-            z_copy(m, k).start()
-            return carry
-
-        lax.fori_loop(lo, hi, body, 0)
-
-    def phase_two(rin, rout, wbuf, obuf, wob, xbuf, mixed):
-        d_blk = 64
-        sub = 256 // heads
-        blocks = model // d_blk
-        row = lax.broadcasted_iota(jnp.int32, (256, 256), 0)
-        col = lax.broadcasted_iota(jnp.int32, (256, 256), 1)
-        pick = jnp.where(col == (row % sub) * heads + row // sub, 1.0, 0.0).astype(BF16)
-
-        def relayout(mat, src_hbm):
-            def in_copy(b):
-                return pltpu.make_async_copy(src_hbm.at[pl.ds(pl.multiple_of(b * d_blk, d_blk), d_blk)], rin.at[b % RIN], rl_in.at[b % RIN])
-
-            def out_copy(b):
-                return pltpu.make_async_copy(rout.at[b % ROUT], wrel_hbm.at[mat, :, pl.ds(pl.multiple_of(b * d_blk, d_blk), d_blk), :], rl_out.at[b % ROUT])
-
-            for b in range(RIN - 1):
-                in_copy(b).start()
-
-            def body(b, carry):
-                in_copy(b).wait()
-
-                @pl.when(b + RIN - 1 < blocks)
-                def _():
-                    in_copy(b + RIN - 1).start()
-
-                @pl.when(b >= ROUT)
-                def _():
-                    out_copy(b - ROUT).wait()
-                for i in range(d_blk // sub):
-                    tile = rin[b % RIN, i * sub:(i + 1) * sub].reshape(sub * heads, head_dim)
-                    moved = jnp.dot(pick, tile, preferred_element_type=F32).astype(BF16)
-                    rout[b % ROUT, :, i * sub:(i + 1) * sub, :] = moved.reshape(heads, sub, head_dim)
-                out_copy(b).start()
-                return carry
-
-            lax.fori_loop(0, blocks, body, 0)
-            for b in range(blocks - ROUT, blocks):
-                out_copy(b).wait()
-
-        finish(0, 0, 4)
-        relayout(0, wq_hbm)
-        finish(0, 4, 6)
-        relayout(1, wk_hbm)
-        finish(0, 6, 8)
-        relayout(2, wv_hbm)
-
+    def phase_two(wbuf, obuf, wob, xbuf, mixed):
         def w_copy(h, mat):
             return pltpu.make_async_copy(wrel_hbm.at[mat, h], wbuf.at[h % WSLOTS, mat], w_sem.at[h % WSLOTS, mat])
 
-        n_out = model // OCOLS
+        n_out = heads * head_dim // OROWS
 
         def o_copy(n):
-            return pltpu.make_async_copy(wo_hbm.at[:, pl.ds(pl.multiple_of(n * OCOLS, OCOLS), OCOLS)], wob.at[n % OSLOTS], o_sem.at[n % OSLOTS])
+            return pltpu.make_async_copy(wo_hbm.at[pl.ds(pl.multiple_of(n * OROWS, OROWS), OROWS)], wob.at[n % 2], o_sem.at[n % 2])
 
         for h in range(WSLOTS - 1):
             for mat in range(3):
                 w_copy(h, mat).start()
-        for n in range(OSLOTS - 1):
-            o_copy(n).start()
+        o_copy(0).start()
 
         qi = lax.broadcasted_iota(jnp.int32, (seq, seq), 0)
         ki = lax.broadcasted_iota(jnp.int32, (seq, seq), 1)
@@ -340,41 +345,46 @@
                 o = jnp.dot(e.astype(BF16), v, preferred_element_type=F32) / total
                 mixed[:, pl.ds(pl.multiple_of(h * head_dim, head_dim), head_dim)] = o.astype(BF16)
                 if not last:
-                    @pl.when((h % 4 == 0) & (h > 0))
-                    def _():
-                        finish(1, h // 4 + 1, h // 4 + 2)
-                return carry
-
-            lax.fori_loop(0, heads, head, 0)
+                    pl.when(h % 4 == 2)(lambda: finish(1, 2 + h // 4, 3 + h // 4))
+                return carry
 
             def proj(n, carry):
-                nn = pl.ds(pl.multiple_of(n * OCOLS, OCOLS), OCOLS)
+                lax.fori_loop(n * heads // n_out, (n + 1) * heads // n_out, head, 0)
                 o_copy(n).wait()
                 if last:
-                    pl.when(n + OSLOTS - 1 < n_out)(lambda: o_copy(n + OSLOTS - 1).start())
+                    pl.when(n + 1 < n_out)(lambda: o_copy(n + 1).start())
                 else:
-                    o_copy((n + OSLOTS - 1) % n_out).start()
-                pr = jnp.dot(mixed[...], wob[n % OSLOTS], preferred_element_type=F32).astype(BF16)
-                obuf[:, nn] = (y_in[m, :, nn].astype(F32) + pr.astype(F32)).astype(BF16)
+                    o_copy((n + 1) % n_out).start()
+                kk = pl.ds(pl.multiple_of(n * OROWS, OROWS), OROWS)
+                for j in range(model // 512):
+                    nn = slice(j * 512, (j + 1) * 512)
+                    part = jnp.dot(mixed[:, kk], wob[n % 2, :, nn], preferred_element_type=F32)
+                    acc[m, :, nn] = jnp.where(n == 0, part, acc[m, :, nn] + part)
                 return carry
 
             lax.fori_loop(0, n_out, proj, 0)
+
+            def residual(k, carry):
+                sl = pl.ds(pl.multiple_of(k * piece, piece), piece)
+                obuf[sl] = (y_in[m, sl].astype(F32) + acc[m, sl].astype(BF16).astype(F32)).astype(BF16)
+                return carry
+
+            lax.fori_loop(0, pieces, residual, 0)
             out_cp = pltpu.make_async_copy(obuf, out_hbm.at[m], misc_sem.at[4])
             out_cp.start()
             out_cp.wait()
 
+        finish(0, 6, 8)
         finish(1, 0, 2)
         attention(0)
-        finish(1, 5, 8)
+        finish(1, 6, 8)
         attention(1)
 
     pl.run_scoped(
         phase_two,
-        pltpu.VMEM((RIN, 64, heads, head_dim), BF16),
-        pltpu.VMEM((ROUT, heads, 64, head_dim), BF16),
         pltpu.VMEM((WSLOTS, 3, model, head_dim), BF16),
         pltpu.VMEM((seq, model), BF16),
-        pltpu.VMEM((OSLOTS, heads * head_dim, OCOLS), BF16),
+        pltpu.VMEM((2, OROWS, model), BF16),
         pltpu.VMEM((seq, model), BF16),
         pltpu.VMEM((seq, heads * head_dim), BF16),
     )
@@ -430,7 +440,7 @@
                 dma((micro, 2)), dma((micro, 2)),
                 dma((micro, pieces)), dma((micro, pieces)),
                 dma((micro, pieces)), dma((micro, pieces)),
-                dma((2, 2)), dma((5,)), dma((WSLOTS, 3)), dma((OSLOTS,)), dma((RIN,)), dma((ROUT,)),
+                dma((3,)), dma((5,)), dma((WSLOTS, 3)), dma((2,)), dma((RIN,)), dma((ROUT,)),
             ],
             compiler_params=pltpu.CompilerParams(collective_id=0, has_side_effects=True, vmem_limit_bytes=67043328),
         )(

time: 193 us -> 182 us (0.943)
  Pallas kernels: 187 us -> 177 us
    pallas_call x1, Pallas kernels: 187 us -> 177 us  [device_step(): pl.pallas_call(functools.partial(boundary_kernel, dims), out_shape=(jax.S...]
where the time goes in v3:
time: 182 us
  Pallas kernels  177 us (97%)
  local copies, waits for them, and re-layouts  3.9 us (2%)
    pallas_call x1, Pallas kernels, device_step(): pl.pallas_call(functools.partial(boundary_kernel, dims), out_shape=(jax.S...  177 us
    unnamed x2, local copies, waits for them, and re-layouts  3.9 us

profile of v3, /device:TPU:0, one launch (start us, length us, event | category | flops | bytes accessed | tf_op | source)
XLA Modules:
  0.0 182.1 jit_solution(689682399779408308)
XLA Ops:
  0.0 0.7 copy.41
  0.8 0.8 fusion.4
  1.5 0.6 select_maximum_fusion.meta
  2.2 176.8 %shard_map.136 = (bf16[2,256,2048]{2,1,0:T(8,128)(2,1)}, bf16[3,16,2048,256]{3,2,1,0:T(8,128)(2,1)}) custom-call(f32[2,48,256]{2,1,0:T(8,128)} %select_maximum_fusion.meta, bf16[2,128,32,2048]{3,2,1,0:T(8,128)(2,1)} %bitcast.26, bf16[2,256,2048]{2,1,0:T(8,128)(2,1)} %bitcast.31, f32[1,2048]{1,0:T(1,128)} %norm_moe.1, f32[1,2048]{1,0:T(1,128)} %norm_attn.1, ...), custom_call_target="tpu_custom_call" | custom-call | tf_op jit(solution)/shard_map/pallas_call | solution.py:422
  179.0 3.2 %copy.43 = bf16[1,2,1,256,2048]{4,3,2,1,0:T(8,128)(2,1)} copy(bf16[1,2,1,256,2048]{4,3,2,1,0:T(8,128)(2,1)} %bitcast.35) | data formatting | bytes 4194304
  (1 shorter events, 0.0 us)

commit v4 on v3

--- a/solution.py
+++ b/solution.py
@@ -19,7 +19,7 @@
 
 def boundary_kernel(dims, meta, rows_hbm, resid_hbm, norm_moe, norm_attn, wg_hbm, wu_hbm, wd_hbm, wq_hbm, wk_hbm, wv_hbm, wo_hbm,
                     out_hbm, wrel_hbm,
-                    meta_all, meta_cols, send_part, recv_part, mine, y_recv, recv_own, acc, y_send, y_in,
+                    meta_all, send_part, recv_part, mine, y_recv, recv_own, acc, y_send, y_in,
                     meta_ss, meta_rs, part_ss, part_rs, own_ss, own_rs, y_ss, y_rs, z_ss, z_rs, row_sem, misc_sem, w_sem, o_sem, rl_in, rl_out):
     micro, seq, model, heads, head_dim, local_experts, cap, top_k, ff, stages = dims
     local_cols = local_experts * cap
@@ -36,15 +36,8 @@
     diag = (1 - chip) * 2 + (1 - core)
     nxt, prv = (stage + 1) % stages, (stage + stages - 1) % stages
 
-    barrier = pltpu.get_barrier_semaphore()
-    for peer in (partner, across, diag):
-        pl.semaphore_signal(barrier, inc=1, device_id={"ep": peer}, device_id_type=MESH)
-    for peer in (nxt, prv):
-        pl.semaphore_signal(barrier, inc=1, device_id={"pp": peer}, device_id_type=MESH)
-    pl.semaphore_wait(barrier, 5)
-
     def meta_copy(rel, peer):
-        return pltpu.make_async_remote_copy(src_ref=meta, dst_ref=meta_all.at[rel - 1], send_sem=meta_ss.at[rel - 1], recv_sem=meta_rs.at[rel - 1], device_id={"ep": peer}, device_id_type=MESH)
+        return pltpu.make_async_remote_copy(src_ref=meta, dst_ref=meta_all.at[rel], send_sem=meta_ss.at[rel - 1], recv_sem=meta_rs.at[rel - 1], device_id={"ep": peer}, device_id_type=MESH)
 
     def part_copy(m, c):
         sl = pl.ds(pl.multiple_of(c * half, half), half)
@@ -61,21 +54,18 @@
     def z_copy(m, k):
         sl = pl.ds(pl.multiple_of(k * piece, piece), piece)
         return pltpu.make_async_remote_copy(src_ref=y_send.at[m, sl], dst_ref=y_in.at[m, sl], send_sem=z_ss.at[m, k], recv_sem=z_rs.at[m, k], device_id={"pp": nxt}, device_id_type=MESH)
-
-    for rel, peer in ((2, across), (3, diag), (1, partner)):
-        meta_copy(rel, peer).start()
 
     def finish(m, lo, hi):
         def body(k, carry):
             sl = pl.ds(pl.multiple_of(k * piece, piece), piece)
             y_copy(m, k).wait()
-            y_send[m, sl] = (acc[m, sl] + y_recv[m, sl]).astype(BF16)
+            y_send[m, sl] = (acc[m, sl] + recv_own[m, sl] + y_recv[m, sl]).astype(BF16)
             z_copy(m, k).start()
             return carry
 
         lax.fori_loop(lo, hi, body, 0)
 
-    def phase_one(rbuf, wbuf, wg, wu, wd, xs, hid, resid, spread, pick, rin, rout):
+    def phase_one(rbuf, wbuf, wg, wu, wd, xs, hid, resid, spread, packed, pick, rin, rout):
         def rows_copy(p, ab):
             m = p % 2
             far = 1 - p // 2
@@ -95,15 +85,54 @@
         for cp in (res_cp, wg_cp, wu_cp, wd_cp):
             cp.start()
 
-        for m in range(micro):
-            meta_cols[0, m] = meta[m].T
+        barrier = pltpu.get_barrier_semaphore()
+        for peer in (partner, across, diag):
+            pl.semaphore_signal(barrier, inc=1, device_id={"ep": peer}, device_id_type=MESH)
+        for peer in (nxt, prv):
+            pl.semaphore_signal(barrier, inc=1, device_id={"pp": peer}, device_id_type=MESH)
+        pl.semaphore_wait(barrier, 5)
+
+        for rel, peer in ((2, across), (3, diag), (1, partner)):
+            meta_copy(rel, peer).start()
+
+        for cp in (res_cp, wg_cp, wu_cp, wd_cp):
+            cp.wait()
+
+        def shared(m, carry):
+            def norm(k, carry):
+                sl = pl.ds(pl.multiple_of(k * piece, piece), piece)
+                v = resid[m, sl].astype(F32)
+                inv = lax.rsqrt(jnp.mean(v * v, axis=-1, keepdims=True) + EPSILON)
+                xs[sl] = (v * inv * norm_moe[...]).astype(BF16)
+                return carry
+
+            lax.fori_loop(0, pieces, norm, 0)
+
+            def up(n, carry):
+                nn = pl.ds(pl.multiple_of(n * 256, 256), 256)
+                g = jnp.dot(xs[...], wg[:, nn], preferred_element_type=F32)
+                u = jnp.dot(xs[...], wu[:, nn], preferred_element_type=F32)
+                hid[:, nn] = (g * (1.0 / (1.0 + jnp.exp(-g))) * u).astype(BF16)
+                return carry
+
+            lax.fori_loop(0, ff // 256, up, 0)
+            def down(n, carry):
+                nn = pl.ds(pl.multiple_of(n * 256, 256), 256)
+                s = jnp.dot(hid[...], wd[:, nn], preferred_element_type=F32).astype(BF16)
+                acc[m, :, nn] = resid[m, :, nn].astype(F32) + s.astype(F32)
+                return carry
+
+            lax.fori_loop(0, model // 256, down, 0)
+            return carry
+
+        lax.fori_loop(0, micro, shared, 0)
+
+        meta_all[0] = meta[...]
         for rel, peer in ((2, across), (3, diag), (1, partner)):
             meta_copy(rel, peer).wait()
-            for m in range(micro):
-                meta_cols[rel, m] = meta_all[rel - 1, m].T
 
         group = 32
-        lane = (lax.broadcasted_iota(jnp.int32, (group, local_experts), 1) + local_experts * me).astype(F32)
+        expert = (lax.broadcasted_iota(jnp.int32, (local_experts, half), 0) + local_experts * me).astype(F32)
         lane_slot = (lax.broadcasted_iota(jnp.int32, (group, 256), 1) % cap).astype(F32)
         from_row = lax.broadcasted_iota(jnp.int32, (local_experts, 256), 0)
         to_col = lax.broadcasted_iota(jnp.int32, (local_experts, 256), 1) // cap
@@ -131,57 +160,80 @@
         for b in range(RIN - 2):
             in_copy(wq_hbm, b).start()
 
+        def gate_table(u):
+            u = jnp.minimum(u, 15)
+            p, c, ab = u // 4, (u // 2) % 2, u % 2
+            rel = (1 - ab) + 2 * (1 - p // 2)
+            tab = meta_all[rel, p % 2, :, pl.ds(pl.multiple_of(c * half, half), half)]
+            gates, slots = [], []
+            for r in range(local_experts // 32):
+                ids = expert[r * 32:(r + 1) * 32]
+                gate = jnp.zeros((32, half), F32)
+                slot = jnp.zeros((32, half), F32)
+                for j in range(top_k):
+                    hit = tab[j:j + 1] == ids
+                    gate = jnp.where(hit, tab[GATE_ROW + j:GATE_ROW + j + 1], gate)
+                    slot = jnp.where(hit, tab[SLOT_ROW + j:SLOT_ROW + j + 1], slot)
+                gates.append(gate)
+                slots.append(slot)
+            gate = jnp.concatenate(gates, axis=0).T
+            slot = jnp.concatenate(slots, axis=0).T
+            hi = jnp.minimum(gate, BF16_MAX).astype(BF16)
+            rest = gate - hi.astype(F32)
+            mid = rest.astype(BF16)
+            low = (rest - mid.astype(F32)).astype(BF16)
+            for part, value in enumerate((slot.astype(BF16), hi, mid, low)):
+                packed[:, part] = value.reshape(half // group, group, local_experts)
+
+        def spread_group(to, r):
+            mix = packed[r].reshape(4 * group, local_experts)
+            for kb in range(local_cols // 256):
+                wide = jnp.dot(mix, spread[kb], preferred_element_type=F32)
+                keep = wide[0:group] == lane_slot
+                for part in range(3):
+                    term = jnp.where(keep, wide[(part + 1) * group:(part + 2) * group], 0.0)
+                    at = pl.ds(pl.multiple_of(part * half + r * group, group), group)
+                    wbuf[to, at, kb * 256:(kb + 1) * 256] = term.astype(BF16)
+
+        def first_spread(r, carry):
+            spread_group(0, r)
+            return carry
+
+        gate_table(0)
+        lax.fori_loop(0, half // group, first_spread, 0)
+        gate_table(1)
+
         def partial_sum(p, c, ab, dst, ride=False):
             m = p % 2
-            far = 1 - p // 2
-            rel = (1 + 2 * far) if ab == 0 else 2 * far
             tok = pl.ds(pl.multiple_of(c * half, half), half)
-            table = meta_cols[rel, m, tok, :]
-
-            for r in range(half // group):
-                rows = slice(r * group, (r + 1) * group)
-                gate = jnp.zeros((group, local_experts), F32)
-                slot = jnp.zeros((group, local_experts), F32)
-                for j in range(top_k):
-                    hit = table[rows, j:j + 1] == lane
-                    gate = jnp.where(hit, table[rows, GATE_ROW + j:GATE_ROW + j + 1], gate)
-                    slot = jnp.where(hit, table[rows, SLOT_ROW + j:SLOT_ROW + j + 1], slot)
-                hi = jnp.minimum(gate, BF16_MAX).astype(BF16)
-                rest = gate - hi.astype(F32)
-                mid = rest.astype(BF16)
-                low = (rest - mid.astype(F32)).astype(BF16)
-                packed = jnp.concatenate([slot.astype(BF16), hi, mid, low], axis=0)
-                for kb in range(local_cols // 256):
-                    wide = jnp.dot(packed, spread[kb], preferred_element_type=F32)
-                    keep = wide[0:group] == lane_slot
-                    for part in range(3):
-                        term = jnp.where(keep, wide[(part + 1) * group:(part + 2) * group], 0.0)
-                        wbuf[ab, part * half + r * group:part * half + (r + 1) * group, kb * 256:(kb + 1) * 256] = term.astype(BF16)
 
             def mul(n, carry):
-                nn = pl.ds(pl.multiple_of(n * 512, 512), 512)
                 b0 = 2 * (((2 * p + c - 2) * 2 + ab) * (model // 512) + n)
                 if ride:
                     for b in (b0, b0 + 1):
                         in_copy(wq_hbm, b).wait()
                         in_start(b + RIN - 2)
-
-                        @pl.when(b >= ROUT)
-                        def _():
-                            out_copy(b - ROUT).wait()
-                rr = rbuf[(2 * p + ab) % 3, :, :, nn].reshape(local_cols, 512)
-                d = jnp.dot(wbuf[ab], rr, preferred_element_type=F32)
-                dst[m, tok, nn] = d[0:half] + d[half:2 * half] + d[2 * half:3 * half]
-                if ride:
-                    for b in (b0, b0 + 1):
+                        pl.when(b >= ROUT)(lambda: out_copy(b - ROUT).wait())
+                for part in range(2):
+                    nn = pl.ds(pl.multiple_of(n * 512 + part * 256, 256), 256)
+                    rr = rbuf[(2 * p + ab) % 3, :, :, nn].reshape(local_cols, 256)
+                    d = jnp.dot(wbuf[ab], rr, preferred_element_type=F32)
+                    d = d[0:half] + d[half:2 * half] + d[2 * half:3 * half]
+                    dst[m, tok, nn] = dst[m, tok, nn] + d if dst is acc else d
+                    if ride:
+                        b = b0 + part
                         for i in range(D_BLK // sub):
                             tile = rin[b % RIN, i * sub:(i + 1) * sub].reshape(sub * heads, head_dim)
                             moved = jnp.dot(pick[...], tile, preferred_element_type=F32).astype(BF16)
                             rout[b % ROUT, :, i * sub:(i + 1) * sub, :] = moved.reshape(heads, sub, head_dim)
-                        out_copy(b).start()
+                spread_group(1 - ab, n)
+                if ride:
+                    out_copy(b0).start()
+                    out_copy(b0 + 1).start()
                 return carry
 
             lax.fori_loop(0, model // 512, mul, 0)
+            gate_table(2 * (2 * p + c) + ab + 2)
 
         def pair_step(q, ride):
             p, c = q // 2, q % 2
@@ -215,35 +267,6 @@
             if ride:
                 pl.when(p >= 2)(lambda: partial_sum(p, c, 1, acc, ride))
 
-        def shared(m):
-            def norm(k, carry):
-                sl = pl.ds(pl.multiple_of(k * piece, piece), piece)
-                v = resid[m, sl].astype(F32)
-                inv = lax.rsqrt(jnp.mean(v * v, axis=-1, keepdims=True) + EPSILON)
-                xs[sl] = (v * inv * norm_moe[...]).astype(BF16)
-                return carry
-
-            lax.fori_loop(0, pieces, norm, 0)
-
-            def up(n, carry):
-                nn = pl.ds(pl.multiple_of(n * 256, 256), 256)
-                g = jnp.dot(xs[...], wg[:, nn], preferred_element_type=F32)
-                u = jnp.dot(xs[...], wu[:, nn], preferred_element_type=F32)
-                hid[:, nn] = (g * (1.0 / (1.0 + jnp.exp(-g))) * u).astype(BF16)
-                return carry
-
-            lax.fori_loop(0, ff // 256, up, 0)
-            for c in range(2):
-                own_copy(m, c).wait()
-
-            def down(n, carry):
-                nn = pl.ds(pl.multiple_of(n * 256, 256), 256)
-                s = jnp.dot(hid[...], wd[:, nn], preferred_element_type=F32).astype(BF16)
-                acc[m, :, nn] = (resid[m, :, nn].astype(F32) + s.astype(F32)) + (acc[m, :, nn] + recv_own[m, :, nn])
-                return carry
-
-            lax.fori_loop(0, model // 256, down, 0)
-
         def stage_step(t, carry):
             def riding(c, inner):
                 pair_step(2 * t + c, True)
@@ -253,15 +276,9 @@
 
             @pl.when(t >= 2)
             def _():
-                @pl.when(t == 2)
-                def _():
-                    for cp in (res_cp, wg_cp, wu_cp, wd_cp):
-                        cp.wait()
-                shared(t - 2)
-
-                @pl.when(t == 2)
-                def _():
-                    finish(0, 0, 6)
+                for c in range(2):
+                    own_copy(t - 2, c).wait()
+                pl.when(t == 2)(lambda: finish(0, 0, 6))
             return carry
 
         def first(q, carry):
@@ -284,12 +301,13 @@
         pltpu.VMEM((seq, ff), BF16),
         pltpu.VMEM((micro, seq, model), BF16),
         pltpu.VMEM((local_cols // 256, local_experts, 256), BF16),
+        pltpu.VMEM((4, 4, seq // 8, local_experts), BF16),
         pltpu.VMEM((256, 256), BF16),
         pltpu.VMEM((RIN, D_BLK, heads, head_dim), BF16),
         pltpu.VMEM((ROUT, heads, D_BLK, head_dim), BF16),
     )
 
-    def phase_two(wbuf, obuf, wob, xbuf, mixed):
+    def phase_two(wbuf, obuf, wob, xbuf, mixed, qkv):
         def w_copy(h, mat):
             return pltpu.make_async_copy(wrel_hbm.at[mat, h], wbuf.at[h % WSLOTS, mat], w_sem.at[h % WSLOTS, mat])
 
@@ -321,6 +339,18 @@
 
             lax.fori_loop(0, pieces, norm, 0)
 
+            def softmax_head(h, between):
+                s = lax.dot_general(qkv[0], qkv[1], (((1,), (1,)), ((), ())), preferred_element_type=F32) * scale
+                value = qkv[2]
+                between()
+                s = jnp.where(causal, s, -1e30)
+                e = jnp.exp(s - jnp.max(s, axis=-1, keepdims=True))
+                total = jnp.sum(e, axis=-1, keepdims=True)
+                between()
+                o = jnp.dot(e.astype(BF16), value, preferred_element_type=F32) / total
+                between()
+                mixed[:, pl.ds(pl.multiple_of(h * head_dim, head_dim), head_dim)] = o.astype(BF16)
+
             def head(h, carry):
                 slot = h % WSLOTS
                 for mat in range(3):
@@ -335,21 +365,20 @@
                 else:
                     prefetch()
                 x = xbuf[...]
-                q = jnp.dot(x, wbuf[slot, 0], preferred_element_type=F32).astype(BF16)
-                k = jnp.dot(x, wbuf[slot, 1], preferred_element_type=F32).astype(BF16)
-                v = jnp.dot(x, wbuf[slot, 2], preferred_element_type=F32).astype(BF16)
-                s = lax.dot_general(q, k, (((1,), (1,)), ((), ())), preferred_element_type=F32) * scale
-                s = jnp.where(causal, s, -1e30)
-                e = jnp.exp(s - jnp.max(s, axis=-1, keepdims=True))
-                total = jnp.sum(e, axis=-1, keepdims=True)
-                o = jnp.dot(e.astype(BF16), v, preferred_element_type=F32) / total
-                mixed[:, pl.ds(pl.multiple_of(h * head_dim, head_dim), head_dim)] = o.astype(BF16)
+                fresh = []
+
+                def project():
+                    mat = len(fresh)
+                    fresh.append(jnp.dot(x, wbuf[slot, mat], preferred_element_type=F32).astype(BF16))
+
+                softmax_head(jnp.maximum(h - 1, 0), project)
+                for mat in range(3):
+                    qkv[mat] = fresh[mat]
                 if not last:
-                    pl.when(h % 4 == 2)(lambda: finish(1, 2 + h // 4, 3 + h // 4))
+                    pl.when((h % 3 == 2) & (h < 12))(lambda: finish(1, 4 + h // 3, 5 + h // 3))
                 return carry
 
             def proj(n, carry):
-                lax.fori_loop(n * heads // n_out, (n + 1) * heads // n_out, head, 0)
                 o_copy(n).wait()
                 if last:
                     pl.when(n + 1 < n_out)(lambda: o_copy(n + 1).start())
@@ -362,6 +391,8 @@
                     acc[m, :, nn] = jnp.where(n == 0, part, acc[m, :, nn] + part)
                 return carry
 
+            lax.fori_loop(0, heads, head, 0)
+            softmax_head(heads - 1, lambda: None)
             lax.fori_loop(0, n_out, proj, 0)
 
             def residual(k, carry):
@@ -374,10 +405,10 @@
             out_cp.start()
             out_cp.wait()
 
+        qkv[...] = jnp.zeros_like(qkv)
         finish(0, 6, 8)
-        finish(1, 0, 2)
+        finish(1, 0, 4)
         attention(0)
-        finish(1, 6, 8)
         attention(1)
 
     pl.run_scoped(
@@ -387,6 +418,7 @@
         pltpu.VMEM((2, OROWS, model), BF16),
         pltpu.VMEM((seq, model), BF16),
         pltpu.VMEM((seq, heads * head_dim), BF16),
+        pltpu.VMEM((3, seq, head_dim), BF16),
     )
 
 
@@ -425,8 +457,7 @@
             in_specs=[vmem, hbm, hbm, vmem, vmem] + [hbm] * 7,
             out_specs=(hbm, hbm),
             scratch_shapes=[
-                pltpu.VMEM((3, micro, META_ROWS, seq), F32),
-                pltpu.VMEM((4, micro, seq, META_ROWS), F32),
+                pltpu.VMEM((4, micro, META_ROWS, seq), F32),
                 pltpu.VMEM((micro, seq, model), F32),
                 pltpu.VMEM((micro, seq, model), F32),
                 pltpu.VMEM((micro, seq, model), F32),

time: 182 us -> 166 us (0.912)
  Pallas kernels: 177 us -> 160 us
    pallas_call x1, Pallas kernels: 177 us -> 160 us  [device_step(): pl.pallas_call(functools.partial(boundary_kernel, dims), out_shape=(jax.S...]
where the time goes in v4:
time: 166 us
  Pallas kernels  160 us (96%)
  local copies, waits for them, and re-layouts  3.9 us (2%)
    pallas_call x1, Pallas kernels, device_step(): pl.pallas_call(functools.partial(boundary_kernel, dims), out_shape=(jax.S...  160 us
    unnamed x2, local copies, waits for them, and re-layouts  3.9 us

profile of v4, /device:TPU:0, one launch (start us, length us, event | category | flops | bytes accessed | tf_op | source)
XLA Modules:
  0.0 165.7 jit_solution(14686176474509558536)
XLA Ops:
  0.0 0.7 copy.41
  0.8 0.8 fusion.4
  1.5 0.6 select_maximum_fusion.meta
  2.2 160.3 %shard_map.136 = (bf16[2,256,2048]{2,1,0:T(8,128)(2,1)}, bf16[3,16,2048,256]{3,2,1,0:T(8,128)(2,1)}) custom-call(f32[2,48,256]{2,1,0:T(8,128)} %select_maximum_fusion.meta, bf16[2,128,32,2048]{3,2,1,0:T(8,128)(2,1)} %bitcast.26, bf16[2,256,2048]{2,1,0:T(8,128)(2,1)} %bitcast.31, f32[1,2048]{1,0:T(1,128)} %norm_moe.1, f32[1,2048]{1,0:T(1,128)} %norm_attn.1, ...), custom_call_target="tpu_custom_call" | custom-call | tf_op jit(solution)/shard_map/pallas_call | solution.py:454
  162.5 3.2 %copy.43 = bf16[1,2,1,256,2048]{4,3,2,1,0:T(8,128)(2,1)} copy(bf16[1,2,1,256,2048]{4,3,2,1,0:T(8,128)(2,1)} %bitcast.35) | data formatting | bytes 4194304
  (1 shorter events, 0.0 us)

commit v5 on v4

--- a/solution.py
+++ b/solution.py
@@ -14,7 +14,7 @@
 META_ROWS = 48
 GATE_ROW = 16
 SLOT_ROW = 32
-RIN, ROUT, D_BLK, WSLOTS, OROWS = 6, 4, 64, 4, 1024
+RIN, ROUT, RSTEP, D_BLK, WSLOTS, OSLOTS, OROWS = 8, 6, 2, 64, 6, 4, 512
 
 
 def boundary_kernel(dims, meta, rows_hbm, resid_hbm, norm_moe, norm_attn, wg_hbm, wu_hbm, wd_hbm, wq_hbm, wk_hbm, wv_hbm, wo_hbm,
@@ -157,7 +157,7 @@
             at = pl.ds(pl.multiple_of(b % mat_blocks * D_BLK, D_BLK), D_BLK)
             return pltpu.make_async_copy(rout.at[b % ROUT], wrel_hbm.at[b // mat_blocks, :, at, :], rl_out.at[b % ROUT])
 
-        for b in range(RIN - 2):
+        for b in range(RIN - RSTEP):
             in_copy(wq_hbm, b).start()
 
         def gate_table(u):
@@ -207,15 +207,18 @@
             m = p % 2
             tok = pl.ds(pl.multiple_of(c * half, half), half)
 
+            steps = model // (256 * RSTEP)
+
             def mul(n, carry):
-                b0 = 2 * (((2 * p + c - 2) * 2 + ab) * (model // 512) + n)
+                b0 = RSTEP * (((2 * p + c - 2) * 2 + ab) * steps + n)
                 if ride:
-                    for b in (b0, b0 + 1):
+                    for part in range(RSTEP):
+                        b = b0 + part
                         in_copy(wq_hbm, b).wait()
-                        in_start(b + RIN - 2)
+                        in_start(b + RIN - RSTEP)
                         pl.when(b >= ROUT)(lambda: out_copy(b - ROUT).wait())
-                for part in range(2):
-                    nn = pl.ds(pl.multiple_of(n * 512 + part * 256, 256), 256)
+                for part in range(RSTEP):
+                    nn = pl.ds(pl.multiple_of((n * RSTEP + part) * 256, 256), 256)
                     rr = rbuf[(2 * p + ab) % 3, :, :, nn].reshape(local_cols, 256)
                     d = jnp.dot(wbuf[ab], rr, preferred_element_type=F32)
                     d = d[0:half] + d[half:2 * half] + d[2 * half:3 * half]
@@ -226,13 +229,14 @@
                             tile = rin[b % RIN, i * sub:(i + 1) * sub].reshape(sub * heads, head_dim)
                             moved = jnp.dot(pick[...], tile, preferred_element_type=F32).astype(BF16)
                             rout[b % ROUT, :, i * sub:(i + 1) * sub, :] = moved.reshape(heads, sub, head_dim)
-                spread_group(1 - ab, n)
+                    if part % 2 == 1:
+                        spread_group(1 - ab, n * (RSTEP // 2) + part // 2)
                 if ride:
-                    out_copy(b0).start()
-                    out_copy(b0 + 1).start()
-                return carry
-
-            lax.fori_loop(0, model // 512, mul, 0)
+                    for part in range(RSTEP):
+                        out_copy(b0 + part).start()
+                return carry
+
+            lax.fori_loop(0, steps, mul, 0)
             gate_table(2 * (2 * p + c) + ab + 2)
 
         def pair_step(q, ride):
@@ -269,6 +273,7 @@
 
         def stage_step(t, carry):
             def riding(c, inner):
+                pl.when((t == 3) & (c == 1))(lambda: finish(0, 5, 7))
                 pair_step(2 * t + c, True)
                 return inner
 
@@ -278,7 +283,7 @@
             def _():
                 for c in range(2):
                     own_copy(t - 2, c).wait()
-                pl.when(t == 2)(lambda: finish(0, 0, 6))
+                pl.when(t == 2)(lambda: finish(0, 0, 5))
             return carry
 
         def first(q, carry):
@@ -308,23 +313,27 @@
     )
 
     def phase_two(wbuf, obuf, wob, xbuf, mixed, qkv):
-        def w_copy(h, mat):
-            return pltpu.make_async_copy(wrel_hbm.at[mat, h], wbuf.at[h % WSLOTS, mat], w_sem.at[h % WSLOTS, mat])
+        def w_copy(g, mat):
+            return pltpu.make_async_copy(wrel_hbm.at[mat, g % heads], wbuf.at[g % WSLOTS, mat], w_sem.at[g % WSLOTS, mat])
 
         n_out = heads * head_dim // OROWS
 
         def o_copy(n):
-            return pltpu.make_async_copy(wo_hbm.at[pl.ds(pl.multiple_of(n * OROWS, OROWS), OROWS)], wob.at[n % 2], o_sem.at[n % 2])
-
-        for h in range(WSLOTS - 1):
+            return pltpu.make_async_copy(wo_hbm.at[pl.ds(pl.multiple_of(n * OROWS, OROWS), OROWS)], wob.at[n % OSLOTS], o_sem.at[n % OSLOTS])
+
+        for g in range(WSLOTS - 2):
             for mat in range(3):
-                w_copy(h, mat).start()
-        o_copy(0).start()
+                w_copy(g, mat).start()
+        for n in range(OSLOTS):
+            o_copy(n).start()
 
         qi = lax.broadcasted_iota(jnp.int32, (seq, seq), 0)
         ki = lax.broadcasted_iota(jnp.int32, (seq, seq), 1)
         causal = qi >= ki
         scale = 1.0 / (head_dim ** 0.5)
+
+        def out_copy(m):
+            return pltpu.make_async_copy(obuf, out_hbm.at[m], misc_sem.at[4])
 
         def attention(m):
             last = m == micro - 1
@@ -339,9 +348,8 @@
 
             lax.fori_loop(0, pieces, norm, 0)
 
-            def softmax_head(h, between):
-                s = lax.dot_general(qkv[0], qkv[1], (((1,), (1,)), ((), ())), preferred_element_type=F32) * scale
-                value = qkv[2]
+            def softmax_head(h, query, key, value, between):
+                s = lax.dot_general(query, key, (((1,), (1,)), ((), ())), preferred_element_type=F32) * scale
                 between()
                 s = jnp.where(causal, s, -1e30)
                 e = jnp.exp(s - jnp.max(s, axis=-1, keepdims=True))
@@ -351,49 +359,57 @@
                 between()
                 mixed[:, pl.ds(pl.multiple_of(h * head_dim, head_dim), head_dim)] = o.astype(BF16)
 
-            def head(h, carry):
-                slot = h % WSLOTS
-                for mat in range(3):
-                    w_copy(h, mat).wait()
+            def two_heads(i, carry):
+                g = m * heads + 2 * i
+                for k in range(2):
+                    for mat in range(3):
+                        w_copy(g + k, mat).wait()
 
                 def prefetch():
-                    for mat in range(3):
-                        w_copy((h + WSLOTS - 1) % heads, mat).start()
+                    for k in range(2):
+                        for mat in range(3):
+                            w_copy(g + WSLOTS - 2 + k, mat).start()
 
                 if last:
-                    pl.when(h + WSLOTS - 1 < heads)(prefetch)
+                    pl.when(2 * i + WSLOTS - 2 < heads)(prefetch)
                 else:
-                    prefetch()
+                    pl.when(2 * i < heads)(prefetch)
                 x = xbuf[...]
                 fresh = []
 
                 def project():
-                    mat = len(fresh)
-                    fresh.append(jnp.dot(x, wbuf[slot, mat], preferred_element_type=F32).astype(BF16))
-
-                softmax_head(jnp.maximum(h - 1, 0), project)
+                    k, mat = len(fresh) // 3, len(fresh) % 3
+                    fresh.append(jnp.dot(x, wbuf[(g + k) % WSLOTS, mat], preferred_element_type=F32).astype(BF16))
+
+                softmax_head(jnp.maximum(2 * i - 1, 0), qkv[0], qkv[1], qkv[2], project)
+                softmax_head(2 * i, *fresh, project)
                 for mat in range(3):
-                    qkv[mat] = fresh[mat]
+                    qkv[mat] = fresh[3 + mat]
                 if not last:
-                    pl.when((h % 3 == 2) & (h < 12))(lambda: finish(1, 4 + h // 3, 5 + h // 3))
+                    pl.when((i % 2 == 0) & (i > 0))(lambda: finish(1, 3 + i // 2, 4 + i // 2))
                 return carry
 
             def proj(n, carry):
                 o_copy(n).wait()
-                if last:
-                    pl.when(n + 1 < n_out)(lambda: o_copy(n + 1).start())
-                else:
-                    o_copy((n + 1) % n_out).start()
                 kk = pl.ds(pl.multiple_of(n * OROWS, OROWS), OROWS)
                 for j in range(model // 512):
                     nn = slice(j * 512, (j + 1) * 512)
-                    part = jnp.dot(mixed[:, kk], wob[n % 2, :, nn], preferred_element_type=F32)
+                    part = jnp.dot(mixed[:, kk], wob[n % OSLOTS, :, nn], preferred_element_type=F32)
                     acc[m, :, nn] = jnp.where(n == 0, part, acc[m, :, nn] + part)
-                return carry
-
-            lax.fori_loop(0, heads, head, 0)
-            softmax_head(heads - 1, lambda: None)
+                if last:
+                    pl.when(n + OSLOTS < n_out)(lambda: o_copy(n + OSLOTS).start())
+                else:
+                    o_copy((n + OSLOTS) % n_out).start()
+                return carry
+
+            lax.fori_loop(0, heads // 2, two_heads, 0)
+            if not last:
+                finish(1, 7, 8)
+            softmax_head(heads - 1, qkv[0], qkv[1], qkv[2], lambda: None)
             lax.fori_loop(0, n_out, proj, 0)
+
+            if m > 0:
+                out_copy(m - 1).wait()
 
             def residual(k, carry):
                 sl = pl.ds(pl.multiple_of(k * piece, piece), piece)
@@ -401,21 +417,20 @@
                 return carry
 
             lax.fori_loop(0, pieces, residual, 0)
-            out_cp = pltpu.make_async_copy(obuf, out_hbm.at[m], misc_sem.at[4])
-            out_cp.start()
-            out_cp.wait()
+            out_copy(m).start()
 
         qkv[...] = jnp.zeros_like(qkv)
-        finish(0, 6, 8)
+        finish(0, 7, 8)
         finish(1, 0, 4)
         attention(0)
         attention(1)
+        out_copy(micro - 1).wait()
 
     pl.run_scoped(
         phase_two,
         pltpu.VMEM((WSLOTS, 3, model, head_dim), BF16),
         pltpu.VMEM((seq, model), BF16),
-        pltpu.VMEM((2, OROWS, model), BF16),
+        pltpu.VMEM((OSLOTS, OROWS, model), BF16),
         pltpu.VMEM((seq, model), BF16),
         pltpu.VMEM((seq, heads * head_dim), BF16),
         pltpu.VMEM((3, seq, head_dim), BF16),
@@ -471,7 +486,7 @@
                 dma((micro, 2)), dma((micro, 2)),
                 dma((micro, pieces)), dma((micro, pieces)),
                 dma((micro, pieces)), dma((micro, pieces)),
-                dma((3,)), dma((5,)), dma((WSLOTS, 3)), dma((2,)), dma((RIN,)), dma((ROUT,)),
+                dma((3,)), dma((5,)), dma((WSLOTS, 3)), dma((OSLOTS,)), dma((RIN,)), dma((ROUT,)),
             ],
             compiler_params=pltpu.CompilerParams(collective_id=0, has_side_effects=True, vmem_limit_bytes=67043328),
         )(

time: 166 us -> 157 us (0.946)
  Pallas kernels: 160 us -> 151 us
    pallas_call x1, Pallas kernels: 160 us -> 151 us  [device_step(): pl.pallas_call(functools.partial(boundary_kernel, dims), out_shape=(jax.S...]
where the time goes in v5:
time: 157 us; the launch traced here: 156 us
  Pallas kernels  151 us (96%)
  local copies, waits for them, and re-layouts  3.9 us (2%)
    pallas_call x1, Pallas kernels, device_step(): pl.pallas_call(functools.partial(boundary_kernel, dims), out_shape=(jax.S...  151 us
    unnamed x2, local copies, waits for them, and re-layouts  3.9 us

profile of v5, /device:TPU:0, one launch (start us, length us, event | category | flops | bytes accessed | tf_op | source)
XLA Modules:
  0.0 156.3 jit_solution(7694977924959350754)
XLA Ops:
  0.0 0.7 copy.41
  0.8 0.8 fusion.4
  1.5 0.6 select_maximum_fusion.meta
  2.2 151.0 %shard_map.136 = (bf16[2,256,2048]{2,1,0:T(8,128)(2,1)}, bf16[3,16,2048,256]{3,2,1,0:T(8,128)(2,1)}) custom-call(f32[2,48,256]{2,1,0:T(8,128)} %select_maximum_fusion.meta, bf16[2,128,32,2048]{3,2,1,0:T(8,128)(2,1)} %bitcast.26, bf16[2,256,2048]{2,1,0:T(8,128)(2,1)} %bitcast.31, f32[1,2048]{1,0:T(1,128)} %norm_moe.1, f32[1,2048]{1,0:T(1,128)} %norm_attn.1, ...), custom_call_target="tpu_custom_call" | custom-call | tf_op jit(solution)/shard_map/pallas_call | solution.py:469
  153.1 3.2 %copy.43 = bf16[1,2,1,256,2048]{4,3,2,1,0:T(8,128)(2,1)} copy(bf16[1,2,1,256,2048]{4,3,2,1,0:T(8,128)(2,1)} %bitcast.35) | data formatting | bytes 4194304
  (1 shorter events, 0.0 us)
